TPU v7x, 128 devices: a whole 4x4x4 slice. The times are simulated.
128 devices in a mesh: data: 1, seq: 64 (over z, y, x), dap: 2 (over core).
Axes of the slice: x: 4, y: 4, z: 4, core: 2. Of those that a mesh axis runs over, the one named last changes fastest.
Arguments:
- msa_act: bfloat16 [2048, 512, 64], P(('data', 'seq'), 'dap')
- msa_mask: int32 [2048, 512], P('data')
- pair_act: float32 [512, 512, 128], P(('data', 'dap'))
- ln_gamma: bfloat16 [64], replicated
- ln_beta: bfloat16 [64], replicated
- w_left: bfloat16 [64, 32], replicated
- b_left: bfloat16 [32], replicated
- w_right: bfloat16 [64, 32], replicated
- b_right: bfloat16 [32], replicated
- w_out: bfloat16 [1024, 128], replicated
- b_out: bfloat16 [128], replicated
Outputs:
- output 1: float32 [512, 512, 128], P(('data', 'dap'))
- output 2: bfloat16 [2048, 512, 64], P(('data', 'seq', 'dap'))
All inputs are finite; a program needn't handle non-finite values.
Results may differ from a plain program's by a relative error of at most 0.0127676.
Values are sent between devices in bfloat16 or wider.
A program may use at most 1 GiB of HBM per device.

v0:
```python
import jax
import jax.numpy as jnp
from jax import lax
from jax.sharding import PartitionSpec as P


def block_rows(rows_total, row_width):
    target = max(1, 16384 // row_width)
    return max(divisor for divisor in range(1, min(rows_total, target) + 1) if rows_total % divisor == 0)


def layer_norm(value_a7, ln_gamma, ln_beta):
    act_f32 = value_a7.astype(jnp.float32)
    mean_val = jnp.mean(act_f32, axis=-1, keepdims=True)
    centered = act_f32 - mean_val
    var_val = jnp.mean(centered * centered, axis=-1, keepdims=True)
    normed = centered * lax.rsqrt(var_val + 1e-5)
    return (normed * ln_gamma.astype(jnp.float32) + ln_beta.astype(jnp.float32)).astype(jnp.bfloat16)


def project(normed, weight, bias_vec, mask_f32):
    flat_act = normed.reshape(-1, normed.shape[-1])
    out_f32 = jnp.dot(flat_act, weight, preferred_element_type=jnp.float32) + bias_vec.astype(jnp.float32)
    return (out_f32.reshape(normed.shape[:-1] + (weight.shape[1],)) * mask_f32[:, :, None]).astype(jnp.bfloat16)


def pair_partial(left_proj, right_proj, w_out3):
    n_seq = left_proj.shape[0]
    n_rows = left_proj.shape[1]
    c_hid = left_proj.shape[2]
    n_cols = right_proj.shape[1]
    rows_per = block_rows(n_rows, n_cols)
    left_blocks = jnp.moveaxis(left_proj.reshape(n_seq, n_rows // rows_per, rows_per, c_hid), 1, 0)

    def one_block(left_blk):
        outer_blk = jnp.einsum('sic,sjd->icjd', left_blk, right_proj, preferred_element_type=jnp.float32).astype(jnp.bfloat16)
        return jnp.einsum('icjd,cde->ije', outer_blk, w_out3, preferred_element_type=jnp.float32).astype(jnp.bfloat16)

    return lax.map(one_block, left_blocks).reshape(n_rows, n_cols, w_out3.shape[2])


def solution(mesh):
    dap_size = mesh.shape['dap']
    replicated = P()
    in_specs = (P(('data', 'seq'), 'dap', None), P('data', None), P(('data', 'dap'), None, None), replicated, replicated, replicated, replicated, replicated, replicated, replicated, replicated)
    out_specs = (P(('data', 'dap'), None, None), P(('data', 'seq', 'dap'), None, None))

    def local_fn(array_b7, mask_part, pair_rows, ln_gamma, ln_beta, w_left, b_left, w_right, b_right, w_out, b_out):
        seq_idx = lax.axis_index('seq')
        dap_idx = lax.axis_index('dap')
        local_c7 = lax.all_to_all(array_b7, 'dap', 0, 1, tiled=True)
        n_local = local_c7.shape[0]
        n_rows = pair_rows.shape[0]
        c_hid = w_left.shape[1]
        mask_seq = lax.dynamic_slice_in_dim(mask_part, (seq_idx * dap_size + dap_idx) * n_local, n_local, axis=0).astype(jnp.float32)
        normed = layer_norm(local_c7, ln_gamma, ln_beta)
        left_proj = project(normed, w_left, b_left, mask_seq)
        right_proj = project(normed, w_right, b_right, mask_seq)
        w_out3 = w_out.reshape(c_hid, c_hid, w_out.shape[1])
        partial = pair_partial(left_proj, right_proj, w_out3)
        summed = lax.psum_scatter(partial, 'dap', scatter_dimension=0, tiled=True)
        summed = lax.psum(summed, 'seq')
        mask_bf16 = mask_part.astype(jnp.bfloat16)
        mask_rows = lax.dynamic_slice_in_dim(mask_bf16, dap_idx * n_rows, n_rows, axis=1)
        pair_count = jnp.einsum('si,sj->ij', mask_rows, mask_bf16, preferred_element_type=jnp.float32)
        update = (summed.astype(jnp.float32) + b_out.astype(jnp.float32)) / (1e-3 + pair_count)[:, :, None]
        return pair_rows + update, local_c7

    return jax.shard_map(local_fn, mesh=mesh, in_specs=in_specs, out_specs=out_specs, check_vma=False)
```

profile of v0, /device:TPU:0, one launch (start us, length us, event | category | flops | bytes accessed | tf_op | source)
XLA Modules:
  0.0 828.1 jit_solution(12019452810682029105)
XLA Ops:
  7.2 0.0 copy-start
  7.2 3.6 all-to-all-start
  10.8 0.0 reduce-scatter.5.cloned.1.call-start
  10.8 1.8 all-to-all-done
  12.7 1.0 fusion.19
  13.7 0.0 copy-start.9
  13.7 1.1 bitcast_convert_fusion.1
  14.8 0.8 dynamic-slice_convert_fusion
  15.6 0.1 copy.31
  15.7 1.5 multiply_reduce_fusion
  17.3 2.7 reshape.69
  20.1 1.9 add_convert_fusion
  22.1 0.3 convolution_add_fusion.1
  22.3 2.7 reshape.65
  25.1 6.0 copy.25
  31.1 0.3 convolution_add_fusion
  31.4 0.6 copy.35
  32.0 0.1 fusion.18
  32.2 1.1 copy-done.4
  33.3 1.4 fusion.17
  34.6 307.7 %while.10 = (s32[]{:T(128)}, bf16[16,32,512,128]{3,2,1,0:T(8,128)(2,1)}, bf16[16,16,32,32]{3,1,2,0:T(8,128)(2,1)S(1)}, bf16[16,512,32]{1,0,2:T(8,128)(2,1)S(1)}, bf16[32,32,128]{2,1,0:T(8,128)(2,1)S(1)}, /*index=5*/s32[]{:T(128)}) while((s32[]{:T(128)}, bf16[16,32,512,128]{3,2,1,0:T(8,128)(2,1)}, bf16[16,16,32,32]{3,1,2,0:T(8,128)(2,1)S(1)}, ...), condition=%wide.region_3.4_spmd, body=%wide.region_2.3_spmd.sunk | while | flops 4850712576 | bytes 5112901 | solution.py:39
  34.8 19.2 %fusion.37 = bf16[16,32,512,128]{3,2,1,0:T(8,128)(2,1)} fusion(bf16[16,32,512,128]{3,2,1,0:T(8,128)(2,1)} %get-tuple-element.80, s32[]{:T(128)} %get-tuple-element.79, bf16[16,512,32]{1,0,2:T(8,128)(2,1)S(1)} %get-tuple-element.88, bf16[32,32,128,1]{2,1,0,3:T(8,128)(2,1)S(1)} %bitcast.83, bf16[16,16,32,32]{3,1,2,0:T(8,128)(2,1)S(1)} %get-tuple-element.87), kind=kOutput, calls=%fused_computation.5.clone.1 | convolution fusion | flops 4850712576 | bytes 5112832 | tf_op jit(solution)/shard_map/while/body/eval_jaxpr/icjd,cde->ije/dot_general | solution.py:37
  54.1 19.2 %fusion.37 = bf16[16,32,512,128]{3,2,1,0:T(8,128)(2,1)} fusion(bf16[16,32,512,128]{3,2,1,0:T(8,128)(2,1)} %get-tuple-element.80, s32[]{:T(128)} %get-tuple-element.79, bf16[16,512,32]{1,0,2:T(8,128)(2,1)S(1)} %get-tuple-element.88, bf16[32,32,128,1]{2,1,0,3:T(8,128)(2,1)S(1)} %bitcast.83, bf16[16,16,32,32]{3,1,2,0:T(8,128)(2,1)S(1)} %get-tuple-element.87), kind=kOutput, calls=%fused_computation.5.clone.1 | convolution fusion | flops 4850712576 | bytes 5112832 | tf_op jit(solution)/shard_map/while/body/eval_jaxpr/icjd,cde->ije/dot_general | solution.py:37
  73.3 19.2 %fusion.37 = bf16[16,32,512,128]{3,2,1,0:T(8,128)(2,1)} fusion(bf16[16,32,512,128]{3,2,1,0:T(8,128)(2,1)} %get-tuple-element.80, s32[]{:T(128)} %get-tuple-element.79, bf16[16,512,32]{1,0,2:T(8,128)(2,1)S(1)} %get-tuple-element.88, bf16[32,32,128,1]{2,1,0,3:T(8,128)(2,1)S(1)} %bitcast.83, bf16[16,16,32,32]{3,1,2,0:T(8,128)(2,1)S(1)} %get-tuple-element.87), kind=kOutput, calls=%fused_computation.5.clone.1 | convolution fusion | flops 4850712576 | bytes 5112832 | tf_op jit(solution)/shard_map/while/body/eval_jaxpr/icjd,cde->ije/dot_general | solution.py:37
  92.5 19.2 %fusion.37 = bf16[16,32,512,128]{3,2,1,0:T(8,128)(2,1)} fusion(bf16[16,32,512,128]{3,2,1,0:T(8,128)(2,1)} %get-tuple-element.80, s32[]{:T(128)} %get-tuple-element.79, bf16[16,512,32]{1,0,2:T(8,128)(2,1)S(1)} %get-tuple-element.88, bf16[32,32,128,1]{2,1,0,3:T(8,128)(2,1)S(1)} %bitcast.83, bf16[16,16,32,32]{3,1,2,0:T(8,128)(2,1)S(1)} %get-tuple-element.87), kind=kOutput, calls=%fused_computation.5.clone.1 | convolution fusion | flops 4850712576 | bytes 5112832 | tf_op jit(solution)/shard_map/while/body/eval_jaxpr/icjd,cde->ije/dot_general | solution.py:37
  111.7 19.2 %fusion.37 = bf16[16,32,512,128]{3,2,1,0:T(8,128)(2,1)} fusion(bf16[16,32,512,128]{3,2,1,0:T(8,128)(2,1)} %get-tuple-element.80, s32[]{:T(128)} %get-tuple-element.79, bf16[16,512,32]{1,0,2:T(8,128)(2,1)S(1)} %get-tuple-element.88, bf16[32,32,128,1]{2,1,0,3:T(8,128)(2,1)S(1)} %bitcast.83, bf16[16,16,32,32]{3,1,2,0:T(8,128)(2,1)S(1)} %get-tuple-element.87), kind=kOutput, calls=%fused_computation.5.clone.1 | convolution fusion | flops 4850712576 | bytes 5112832 | tf_op jit(solution)/shard_map/while/body/eval_jaxpr/icjd,cde->ije/dot_general | solution.py:37
  130.9 19.2 %fusion.37 = bf16[16,32,512,128]{3,2,1,0:T(8,128)(2,1)} fusion(bf16[16,32,512,128]{3,2,1,0:T(8,128)(2,1)} %get-tuple-element.80, s32[]{:T(128)} %get-tuple-element.79, bf16[16,512,32]{1,0,2:T(8,128)(2,1)S(1)} %get-tuple-element.88, bf16[32,32,128,1]{2,1,0,3:T(8,128)(2,1)S(1)} %bitcast.83, bf16[16,16,32,32]{3,1,2,0:T(8,128)(2,1)S(1)} %get-tuple-element.87), kind=kOutput, calls=%fused_computation.5.clone.1 | convolution fusion | flops 4850712576 | bytes 5112832 | tf_op jit(solution)/shard_map/while/body/eval_jaxpr/icjd,cde->ije/dot_general | solution.py:37
  150.2 19.2 %fusion.37 = bf16[16,32,512,128]{3,2,1,0:T(8,128)(2,1)} fusion(bf16[16,32,512,128]{3,2,1,0:T(8,128)(2,1)} %get-tuple-element.80, s32[]{:T(128)} %get-tuple-element.79, bf16[16,512,32]{1,0,2:T(8,128)(2,1)S(1)} %get-tuple-element.88, bf16[32,32,128,1]{2,1,0,3:T(8,128)(2,1)S(1)} %bitcast.83, bf16[16,16,32,32]{3,1,2,0:T(8,128)(2,1)S(1)} %get-tuple-element.87), kind=kOutput, calls=%fused_computation.5.clone.1 | convolution fusion | flops 4850712576 | bytes 5112832 | tf_op jit(solution)/shard_map/while/body/eval_jaxpr/icjd,cde->ije/dot_general | solution.py:37
  169.4 19.2 %fusion.37 = bf16[16,32,512,128]{3,2,1,0:T(8,128)(2,1)} fusion(bf16[16,32,512,128]{3,2,1,0:T(8,128)(2,1)} %get-tuple-element.80, s32[]{:T(128)} %get-tuple-element.79, bf16[16,512,32]{1,0,2:T(8,128)(2,1)S(1)} %get-tuple-element.88, bf16[32,32,128,1]{2,1,0,3:T(8,128)(2,1)S(1)} %bitcast.83, bf16[16,16,32,32]{3,1,2,0:T(8,128)(2,1)S(1)} %get-tuple-element.87), kind=kOutput, calls=%fused_computation.5.clone.1 | convolution fusion | flops 4850712576 | bytes 5112832 | tf_op jit(solution)/shard_map/while/body/eval_jaxpr/icjd,cde->ije/dot_general | solution.py:37
  188.6 19.2 %fusion.37 = bf16[16,32,512,128]{3,2,1,0:T(8,128)(2,1)} fusion(bf16[16,32,512,128]{3,2,1,0:T(8,128)(2,1)} %get-tuple-element.80, s32[]{:T(128)} %get-tuple-element.79, bf16[16,512,32]{1,0,2:T(8,128)(2,1)S(1)} %get-tuple-element.88, bf16[32,32,128,1]{2,1,0,3:T(8,128)(2,1)S(1)} %bitcast.83, bf16[16,16,32,32]{3,1,2,0:T(8,128)(2,1)S(1)} %get-tuple-element.87), kind=kOutput, calls=%fused_computation.5.clone.1 | convolution fusion | flops 4850712576 | bytes 5112832 | tf_op jit(solution)/shard_map/while/body/eval_jaxpr/icjd,cde->ije/dot_general | solution.py:37
  207.8 19.2 %fusion.37 = bf16[16,32,512,128]{3,2,1,0:T(8,128)(2,1)} fusion(bf16[16,32,512,128]{3,2,1,0:T(8,128)(2,1)} %get-tuple-element.80, s32[]{:T(128)} %get-tuple-element.79, bf16[16,512,32]{1,0,2:T(8,128)(2,1)S(1)} %get-tuple-element.88, bf16[32,32,128,1]{2,1,0,3:T(8,128)(2,1)S(1)} %bitcast.83, bf16[16,16,32,32]{3,1,2,0:T(8,128)(2,1)S(1)} %get-tuple-element.87), kind=kOutput, calls=%fused_computation.5.clone.1 | convolution fusion | flops 4850712576 | bytes 5112832 | tf_op jit(solution)/shard_map/while/body/eval_jaxpr/icjd,cde->ije/dot_general | solution.py:37
  227.0 19.2 %fusion.37 = bf16[16,32,512,128]{3,2,1,0:T(8,128)(2,1)} fusion(bf16[16,32,512,128]{3,2,1,0:T(8,128)(2,1)} %get-tuple-element.80, s32[]{:T(128)} %get-tuple-element.79, bf16[16,512,32]{1,0,2:T(8,128)(2,1)S(1)} %get-tuple-element.88, bf16[32,32,128,1]{2,1,0,3:T(8,128)(2,1)S(1)} %bitcast.83, bf16[16,16,32,32]{3,1,2,0:T(8,128)(2,1)S(1)} %get-tuple-element.87), kind=kOutput, calls=%fused_computation.5.clone.1 | convolution fusion | flops 4850712576 | bytes 5112832 | tf_op jit(solution)/shard_map/while/body/eval_jaxpr/icjd,cde->ije/dot_general | solution.py:37
  246.2 19.2 %fusion.37 = bf16[16,32,512,128]{3,2,1,0:T(8,128)(2,1)} fusion(bf16[16,32,512,128]{3,2,1,0:T(8,128)(2,1)} %get-tuple-element.80, s32[]{:T(128)} %get-tuple-element.79, bf16[16,512,32]{1,0,2:T(8,128)(2,1)S(1)} %get-tuple-element.88, bf16[32,32,128,1]{2,1,0,3:T(8,128)(2,1)S(1)} %bitcast.83, bf16[16,16,32,32]{3,1,2,0:T(8,128)(2,1)S(1)} %get-tuple-element.87), kind=kOutput, calls=%fused_computation.5.clone.1 | convolution fusion | flops 4850712576 | bytes 5112832 | tf_op jit(solution)/shard_map/while/body/eval_jaxpr/icjd,cde->ije/dot_general | solution.py:37
  265.5 19.2 %fusion.37 = bf16[16,32,512,128]{3,2,1,0:T(8,128)(2,1)} fusion(bf16[16,32,512,128]{3,2,1,0:T(8,128)(2,1)} %get-tuple-element.80, s32[]{:T(128)} %get-tuple-element.79, bf16[16,512,32]{1,0,2:T(8,128)(2,1)S(1)} %get-tuple-element.88, bf16[32,32,128,1]{2,1,0,3:T(8,128)(2,1)S(1)} %bitcast.83, bf16[16,16,32,32]{3,1,2,0:T(8,128)(2,1)S(1)} %get-tuple-element.87), kind=kOutput, calls=%fused_computation.5.clone.1 | convolution fusion | flops 4850712576 | bytes 5112832 | tf_op jit(solution)/shard_map/while/body/eval_jaxpr/icjd,cde->ije/dot_general | solution.py:37
  284.7 19.2 %fusion.37 = bf16[16,32,512,128]{3,2,1,0:T(8,128)(2,1)} fusion(bf16[16,32,512,128]{3,2,1,0:T(8,128)(2,1)} %get-tuple-element.80, s32[]{:T(128)} %get-tuple-element.79, bf16[16,512,32]{1,0,2:T(8,128)(2,1)S(1)} %get-tuple-element.88, bf16[32,32,128,1]{2,1,0,3:T(8,128)(2,1)S(1)} %bitcast.83, bf16[16,16,32,32]{3,1,2,0:T(8,128)(2,1)S(1)} %get-tuple-element.87), kind=kOutput, calls=%fused_computation.5.clone.1 | convolution fusion | flops 4850712576 | bytes 5112832 | tf_op jit(solution)/shard_map/while/body/eval_jaxpr/icjd,cde->ije/dot_general | solution.py:37
  303.9 19.2 %fusion.37 = bf16[16,32,512,128]{3,2,1,0:T(8,128)(2,1)} fusion(bf16[16,32,512,128]{3,2,1,0:T(8,128)(2,1)} %get-tuple-element.80, s32[]{:T(128)} %get-tuple-element.79, bf16[16,512,32]{1,0,2:T(8,128)(2,1)S(1)} %get-tuple-element.88, bf16[32,32,128,1]{2,1,0,3:T(8,128)(2,1)S(1)} %bitcast.83, bf16[16,16,32,32]{3,1,2,0:T(8,128)(2,1)S(1)} %get-tuple-element.87), kind=kOutput, calls=%fused_computation.5.clone.1 | convolution fusion | flops 4850712576 | bytes 5112832 | tf_op jit(solution)/shard_map/while/body/eval_jaxpr/icjd,cde->ije/dot_general | solution.py:37
  323.1 19.2 %fusion.37 = bf16[16,32,512,128]{3,2,1,0:T(8,128)(2,1)} fusion(bf16[16,32,512,128]{3,2,1,0:T(8,128)(2,1)} %get-tuple-element.80, s32[]{:T(128)} %get-tuple-element.79, bf16[16,512,32]{1,0,2:T(8,128)(2,1)S(1)} %get-tuple-element.88, bf16[32,32,128,1]{2,1,0,3:T(8,128)(2,1)S(1)} %bitcast.83, bf16[16,16,32,32]{3,1,2,0:T(8,128)(2,1)S(1)} %get-tuple-element.87), kind=kOutput, calls=%fused_computation.5.clone.1 | convolution fusion | flops 4850712576 | bytes 5112832 | tf_op jit(solution)/shard_map/while/body/eval_jaxpr/icjd,cde->ije/dot_general | solution.py:37
  342.3 0.0 reduce-scatter.5.cloned.1.call-update
  342.3 0.0 all-reduce.3.cloned.1.call-start
  342.4 82.0 %reduce-scatter.5.cloned.1.call-done = bf16[256,512,128]{2,1,0:T(8,128)(2,1)} async-done(((bf16[512,512,128]{2,1,0:T(8,128)(2,1)}), bf16[256,512,128]{2,1,0:T(8,128)(2,1)}) %reduce-scatter.5.cloned.1.call-update) | async-done | bytes 33554448
  424.4 0.0 all-reduce.3.cloned.1.call-update
  424.4 0.0 copy-start.3
  424.5 2.8 convert_element_type.65
  427.3 1.1 copy.42
  428.4 1.5 all_to_all.16
  429.9 0.7 convolution_add_fusion.2
  430.7 336.1 %all-reduce.3.cloned.1.call-done = bf16[256,512,128]{2,1,0:T(8,128)(2,1)} async-done(((bf16[256,512,128]{2,1,0:T(8,128)(2,1)}), bf16[256,512,128]{2,1,0:T(8,128)(2,1)}) %all-reduce.3.cloned.1.call-update) | async-done | bytes 33554448 | tf_op jit(solution)/shard_map/psum | solution.py:62
  766.8 54.5 %divide_add_fusion = f32[256,512,128]{2,1,0:T(8,128)} fusion(f32[256,512,128]{2,1,0:T(8,128)} %param.15, bf16[256,512,128]{2,1,0:T(8,128)(2,1)} %all-reduce.3.cloned.1.call-done, f32[256,512]{1,0:T(8,128)S(1)} %convolution_add_fusion.2, f32[128]{0:T(128)S(1)} %convert_element_type.64), kind=kLoop, calls=%fused_computation.11 | loop fusion | flops 67108864 | bytes 168296960 | tf_op jit(solution)/shard_map/add | solution.py:67
  (30 shorter events, 0.2 us)
Async XLA Ops:
  7.2 14.9 %copy-start = (bf16[64,32]{0,1:T(8,128)(2,1)S(1)}, bf16[64,32]{0,1:T(8,128)(2,1)}, u32[]{:S(2)}) copy-start(bf16[64,32]{0,1:T(8,128)(2,1)} %param.18) | copy-start | bytes 12292
  7.2 5.5 all-to-all-start
  10.8 413.6 %reduce-scatter.5.cloned.1.call-start = ((), (), s32[]{:S(2)}) async-start(), calls=%async_computation.3 | async-start | bytes 100663296
  12.7 7.4 copy-start.2
  13.7 6.4 copy-start.7
  13.7 6.4 copy-start.8
  13.7 6.4 copy-start.9
  25.1 6.0 copy-start.10
  25.1 6.0 copy-start.5
  31.1 2.2 copy-start.4
  32.0 2.6 copy-start.6
  342.3 424.4 %all-reduce.3.cloned.1.call-start = ((), (), s32[]{:S(2)}) async-start(), calls=%async_computation.2 | async-start | bytes 67108864 | tf_op jit(solution)/shard_map/psum | solution.py:62
  424.4 2.9 copy-start.3
  424.4 4.0 copy-start.11
  766.8 54.5 %copy-start.1 = (bf16[64,32]{0,1:T(8,128)(2,1)S(1)}, bf16[64,32]{0,1:T(8,128)(2,1)}, u32[]{:S(2)}) copy-start(bf16[64,32]{0,1:T(8,128)(2,1)} %param.18) | copy-start | bytes 12292
Sparse Core Ops, SparseCore 0:
  342.5 81.8 reduce-scatter.4
  430.2 336.4 all-reduce.2
where the time goes:
time: 829 us; the launch traced here: 828 us
  waiting for transfers between devices  420 us (51%)
  matrix products  309 us (37%)
  other arithmetic  65.2 us (8%)
  local copies, waits for them, and re-layouts  15.9 us (2%)
  between operations  14.3 us (2%)
    psum x1, waiting for transfers between devices, local_fn(): summed = lax.psum(summed, 'seq')  336 us
    dot_general x16, matrix products, one_block(): jnp.einsum('icjd,cde->ije', outer_blk, w_out3, preferred_element_type=jnp...  307 us
    unnamed x3, waiting for transfers between devices  82 us
    add x1, other arithmetic, local_fn(): return (pair_rows + update, local_c7)  54.5 us
  transfers between devices with their start and end apart: 3, of which 3 were waited for; matrix products, arithmetic and copies ran while one was open for 1% of the time, Pallas kernels for 0%

commit v1 on v0

v1 whole, which is shorter than its diff:
```python
import functools

import jax
import jax.numpy as jnp
from jax import lax
from jax.experimental import pallas as pl
from jax.experimental.pallas import tpu as pltpu
from jax.sharding import PartitionSpec as P

CHUNKS = 4


def layer_norm(value, ln_gamma, ln_beta):
    act_f32 = value.astype(jnp.float32)
    mean_val = jnp.mean(act_f32, axis=-1, keepdims=True)
    centered = act_f32 - mean_val
    var_val = jnp.mean(centered * centered, axis=-1, keepdims=True)
    normed = centered * lax.rsqrt(var_val + 1e-5)
    return (normed * ln_gamma.astype(jnp.float32) + ln_beta.astype(jnp.float32)).astype(jnp.bfloat16)


def project(normed, weight, bias_vec, mask_f32):
    out_f32 = jnp.einsum('sic,cd->sid', normed, weight, preferred_element_type=jnp.float32)
    out_f32 = out_f32 + bias_vec.astype(jnp.float32)
    return (out_f32 * mask_f32[:, :, None]).astype(jnp.bfloat16)


def update_kernel(rows, chunk, z_ref, g_ref, inv_ref, b_ref, *rest):
    out_ref = rest[-1]
    blk = pl.program_id(0) * 16 + pl.program_id(1) * 4 + chunk
    shift = lax.rem(blk * rows, 128)
    inv = pltpu.roll(inv_ref[...], lax.rem(128 - shift, 128), 1)
    bias = b_ref[...]
    for r in range(rows):
        col = inv[:, r:r + 1]
        for h in range(2):
            for y in range(4):
                j0 = h * 256 + y * 64
                seg = g_ref[0, y, 0, r, h].astype(jnp.float32)
                out_ref[r, j0:j0 + 64, :] = z_ref[r, j0:j0 + 64, :] + (seg + bias) * col[j0:j0 + 64]


def update(chunk, n_chunks, pair_rows, gathered, inv_t, bias, prev):
    rows = 16 // n_chunks
    g = gathered.reshape(4, 4, 4, rows, 2, 64, 128)
    row_map = lambda zi, xi: (zi * 16 + xi * 4 + chunk, 0, 0) if n_chunks == 4 else None
    in_specs = [
        pl.BlockSpec((rows, 512, 128), row_map),
        pl.BlockSpec((1, 4, 1, rows, 2, 64, 128), lambda zi, xi: (zi, 0, xi, 0, 0, 0, 0)),
        pl.BlockSpec((512, 128), lambda zi, xi: (0, (zi * 64 + xi * 16 + chunk * rows) // 128)),
        pl.BlockSpec((1, 128), lambda zi, xi: (0, 0)),
    ]
    args = [pair_rows, g, inv_t, bias]
    aliases = {}
    if prev is not None:
        in_specs.append(pl.BlockSpec(memory_space=pl.ANY))
        args.append(prev)
        aliases = {4: 0}
    return pl.pallas_call(
        functools.partial(update_kernel, rows, chunk),
        grid=(4, 4),
        in_specs=in_specs,
        out_specs=pl.BlockSpec((rows, 512, 128), row_map),
        out_shape=jax.ShapeDtypeStruct(pair_rows.shape, jnp.float32),
        input_output_aliases=aliases,
        cost_estimate=pl.CostEstimate(flops=30_000_000_000, bytes_accessed=40_000_000, transcendentals=0),
        name='update_%d' % chunk,
    )(*args)


def solution(mesh):
    rep = P()
    in_specs = (P(('data', 'seq'), 'dap', None), P('data', None), P(('data', 'dap'), None, None)) + (rep,) * 8
    out_specs = (P(('data', 'dap'), None, None), P(('data', 'seq', 'dap'), None, None))
    rng = range(4)
    zgroups = [[z * 16 + y * 4 + x for z in rng] for y in rng for x in rng]
    ygroups = [[z * 16 + y * 4 + x for y in rng] for z in rng for x in rng]
    xgroups = [[z * 16 + y * 4 + x for x in rng] for z in rng for y in rng]

    def local_fn(msa, mask, pair_rows, ln_gamma, ln_beta, w_left, b_left, w_right, b_right, w_out, b_out):
        seq_idx = lax.axis_index('seq')
        dap_idx = lax.axis_index('dap')
        msa_out = lax.all_to_all(msa, 'dap', 0, 1, tiled=True)
        mask_seq = lax.dynamic_slice(mask, (seq_idx * 32, dap_idx * 256), (32, 256)).astype(jnp.float32)
        normed = layer_norm(msa, ln_gamma, ln_beta)
        left = project(normed, w_left, b_left, mask_seq)
        right = project(normed, w_right, b_right, mask_seq)
        left = lax.all_to_all(left, 'seq', 1, 0, axis_index_groups=zgroups, tiled=True)
        left = lax.all_gather(left, 'seq', axis=0, axis_index_groups=ygroups, tiled=True)
        right = lax.all_to_all(right, 'seq', 1, 0, axis_index_groups=ygroups, tiled=True)
        right = lax.all_gather(right, 'seq', axis=0, axis_index_groups=zgroups, tiled=True)
        right = lax.all_gather(right, 'dap', axis=1, tiled=True)
        right = right.reshape(4, 4, 32, 128, 32).transpose(1, 0, 2, 3, 4).reshape(512, 128, 32)
        w3 = w_out.reshape(32, 32, 128)
        outer = jnp.einsum('sic,sjd->icjd', left, right, preferred_element_type=jnp.float32).astype(jnp.bfloat16)
        partial = jnp.einsum('icjd,cde->ije', outer, w3, preferred_element_type=jnp.float32).astype(jnp.bfloat16)
        parts = lax.all_to_all(partial.reshape(4, 16, 128, 128), 'seq', 0, 0, axis_index_groups=xgroups, tiled=True)
        total = jnp.sum(parts.astype(jnp.float32), axis=0).astype(jnp.bfloat16)

        mask_bf16 = mask.astype(jnp.bfloat16)
        mask_rows = lax.dynamic_slice_in_dim(mask_bf16, dap_idx * 256, 256, axis=1)
        count_t = jnp.einsum('sj,si->ji', mask_bf16, mask_rows, preferred_element_type=jnp.float32)
        inv_t = 1.0 / (1e-3 + count_t)
        bias = b_out.astype(jnp.float32).reshape(1, 128)

        rows = 16 // CHUNKS
        gathered = [lax.all_gather(total[k * rows:(k + 1) * rows], 'seq', axis=0) for k in range(CHUNKS)]
        out = None
        for k in range(CHUNKS):
            out = update(k, CHUNKS, pair_rows, gathered[k], inv_t, bias, out)
        return out, msa_out

    return jax.shard_map(local_fn, mesh=mesh, in_specs=in_specs, out_specs=out_specs, check_vma=False)
```

time: 829 us -> 526 us (0.63)
  matrix products: 309 us -> 24.3 us
  waiting for transfers between devices: 420 us -> 292 us
  Pallas kernels: 0 us -> 85.3 us
  other arithmetic: 65.2 us -> 8.9 us
  blocking collectives: 0 us -> 54.7 us
  local copies, waits for them, and re-layouts: 15.9 us -> 39.4 us
    psum x1 -> x0, waiting for transfers between devices: 336 us -> none  [local_fn(): summed = lax.psum(summed, 'seq')]
    all_gather x0 -> x7, waiting for transfers between devices: none -> 290 us  [the longest x4 238 us: local_fn(): lax.all_gather(total[k * rows:(k + 1) * rows], 'seq', axis=0)]
    dot_general x19 -> x4, matrix products: 309 us -> 24.3 us  [the longest x1 17.1 us: local_fn(): jnp.einsum('icjd,cde->ije', outer, w3, preferred_element_type=jnp.float32)]
    pallas_call x0 -> x4, Pallas kernels: none -> 85.3 us  [update(): pl.pallas_call(functools.partial(update_kernel, rows, chunk), grid=(4, 4)...]
    unnamed x3 -> x7, waiting for transfers between devices: 82 us -> 1.82 us
    all_to_all x0 -> x3, blocking collectives: none -> 54.7 us  [the longest x1 29 us: local_fn(): lax.all_to_all(partial.reshape(4, 16, 128, 128), 'seq', 0, 0, axis_index_...]
    add x1 -> x0, other arithmetic: 54.5 us -> none  [local_fn(): return (pair_rows + update, local_c7)]
    all_gather x0 -> x1, local copies, waits for them, and re-layouts: none -> 9.13 us  [local_fn(): right = lax.all_gather(right, 'dap', axis=1, tiled=True)]
  transfers between devices with their start and end apart: 3 -> 8, of which waited for: 3 -> 6; matrix products, arithmetic and copies ran while one was open for 1% -> 7% of each run, Pallas kernels for 0% -> 12%
where the time goes in v1:
time: 526 us; the launch traced here: 523 us
  waiting for transfers between devices  292 us (56%)
  Pallas kernels  85.3 us (16%)
  blocking collectives  54.7 us (10%)
  local copies, waits for them, and re-layouts  39.4 us (7%)
  matrix products  24.3 us (5%)
  between operations  14.4 us (3%)
  other arithmetic  8.9 us (2%)
    all_gather x4, waiting for transfers between devices, local_fn(): lax.all_gather(total[k * rows:(k + 1) * rows], 'seq', axis=0)  238 us
    pallas_call x4, Pallas kernels, update(): pl.pallas_call(functools.partial(update_kernel, rows, chunk), grid=(4, 4)...  85.3 us
    all_gather x1, waiting for transfers between devices, local_fn(): lax.all_gather(right, 'seq', axis=0, axis_index_groups=zgroups, tiled=True)  34 us
    all_to_all x1, blocking collectives, local_fn(): lax.all_to_all(partial.reshape(4, 16, 128, 128), 'seq', 0, 0, axis_index_...  29 us
    all_gather x1, waiting for transfers between devices, local_fn(): lax.all_gather(left, 'seq', axis=0, axis_index_groups=ygroups, tiled=True)  18.3 us
    dot_general x1, matrix products, local_fn(): jnp.einsum('icjd,cde->ije', outer, w3, preferred_element_type=jnp.float32)  17.1 us
    all_to_all x1, blocking collectives, local_fn(): lax.all_to_all(right, 'seq', 1, 0, axis_index_groups=ygroups, tiled=True)  13.9 us
    all_to_all x1, blocking collectives, local_fn(): lax.all_to_all(left, 'seq', 1, 0, axis_index_groups=zgroups, tiled=True)  11.8 us
  transfers between devices with their start and end apart: 8, of which 6 were waited for; matrix products, arithmetic and copies ran while one was open for 7% of the time, Pallas kernels for 12%

profile of v1, /device:TPU:0, one launch (start us, length us, event | category | flops | bytes accessed | tf_op | source)
XLA Modules:
  0.0 523.3 jit_solution(4816979083404064665)
XLA Ops:
  7.2 0.0 all-gather.14.cloned.1.call-start
  7.3 1.4 convert_reduce_fusion
  8.7 1.6 fusion.12
  10.4 0.8 dynamic-slice_convert_fusion
  11.2 1.8 fusion.27
  13.0 3.0 copy.36
  16.0 2.2 reshape.76
  18.2 13.9 %all_to_all.59 = bf16[4,2,32768]{2,1,0:T(2,128)(2,1)S(1)} all-to-all(bf16[4,2,32768]{2,1,0:T(2,128)(2,1)S(1)} %reshape.76), channel_id=1, replica_groups={{0,8,16,24},{2,10,18,26},{4,12,20,28},{6,14,22,30},{32,40,48,56},{34,42..., dimensions={0} | all-to-all | bytes 1048576 | tf_op jit(solution)/shard_map/all_to_all | solution.py:90
  32.1 1.1 reshape.77
  33.2 2.2 copy.37
  35.4 2.3 copy.38
  37.8 0.0 all-gather.16.cloned.1.call-start
  37.9 34.0 %all-gather.14.cloned.1.call-done = bf16[512,64,32]{0,2,1:T(8,128)(2,1)} async-done(((bf16[128,64,32]{0,2,1:T(8,128)(2,1)}), bf16[512,64,32]{0,2,1:T(8,128)(2,1)}) %all-gather.14.cloned.1.call-update) | async-done | bytes 2097168 | tf_op jit(solution)/shard_map/all_gather | solution.py:91
  71.9 0.0 all-gather.12.cloned.1.call-start
  71.9 1.8 fusion.26
  73.7 3.0 copy.33
  76.7 2.2 reshape.78
  79.0 11.8 %all_to_all.60 = bf16[4,2,32768]{2,1,0:T(2,128)(2,1)S(1)} all-to-all(bf16[4,2,32768]{2,1,0:T(2,128)(2,1)S(1)} %reshape.78), channel_id=1, replica_groups={{0,32,64,96},{2,34,66,98},{4,36,68,100},{6,38,70,102},{8,40,72,104},{10..., dimensions={0} | all-to-all | bytes 1048576 | tf_op jit(solution)/shard_map/all_to_all | solution.py:88
  90.8 1.1 reshape.79
  91.9 2.2 copy.34
  94.1 2.3 copy.35
  96.4 0.2 all-gather.24.cloned.1.call-start
  96.7 9.1 %copy.39 = bf16[512,128,32]{1,2,0:T(8,128)(2,1)} copy(bf16[512,128,32]{0,2,1:T(8,128)(2,1)} %all-gather.16.cloned.1.call-done) | data formatting | bytes 8388608 | tf_op jit(solution)/shard_map/all_gather | solution.py:92
  105.8 5.1 copy.40
  110.9 18.3 %all-gather.12.cloned.1.call-done = bf16[512,64,32]{0,2,1:T(8,128)(2,1)} async-done(((bf16[128,64,32]{0,2,1:T(8,128)(2,1)}), bf16[512,64,32]{0,2,1:T(8,128)(2,1)}) %all-gather.12.cloned.1.call-update) | async-done | bytes 2097168 | tf_op jit(solution)/shard_map/all_gather | solution.py:89
  129.2 17.1 %bitcast_convert_fusion = bf16[64,128,128]{2,1,0:T(8,128)(2,1)} fusion(bf16[512,128,32]{1,2,0:T(8,128)(2,1)} %bitcast.74, bf16[512,64,32]{0,2,1:T(8,128)(2,1)} %all-gather.12.cloned.1.call-done, bf16[32,32,128]{2,1,0:T(8,128)(2,1)S(1)} %bitcast.78), kind=kOutput, calls=%fused_computation.2 | convolution fusion | flops 10746855424 | bytes 8650752 | tf_op jit(solution)/shard_map/icjd,cde->ije/dot_general | solution.py:96
  146.3 29.0 %all_to_all.61 = bf16[4,16,128,128]{3,2,1,0:T(8,128)(2,1)S(1)} all-to-all(bf16[4,16,128,128]{3,2,1,0:T(8,128)(2,1)} %bitcast.77), channel_id=1, replica_groups={{0,2,4,6},{8,10,12,14},{16,18,20,22},{24,26,28,30},{32,34,36,38},{40,42..., dimensions={0} | all-to-all | bytes 4194304 | tf_op jit(solution)/shard_map/all_to_all | solution.py:97
  175.3 0.4 reduce_sum.32
  175.7 0.8 fusion.38
  176.6 0.0 all-gather.22.cloned.1.call-start
  176.6 0.5 all-gather.22.cloned.1.call-update
  177.2 0.0 all-gather.20.cloned.1.call-start
  177.2 0.5 all-gather.20.cloned.1.call-update
  177.8 0.7 all-gather.18.cloned.1.call-update
  178.5 3.8 all-to-all-start.3
  182.3 4.1 convert_element_type.50
  186.4 1.1 copy.60
  187.5 1.5 all_to_all.54
  189.0 0.5 bitcast_convert_fusion.1.b_ref
  189.5 3.6 fusion.29.inv_ref
  193.2 60.7 %all-gather.24.cloned.1.call-done = bf16[256,128,128]{2,1,0:T(8,128)(2,1)} async-done(((bf16[4,128,128]{2,1,0:T(8,128)(2,1)}), bf16[256,128,128]{2,1,0:T(8,128)(2,1)}) %all-gather.24.cloned.1.call-update) | async-done | bytes 8388624 | tf_op jit(solution)/shard_map/all_gather | solution.py:107
  253.9 21.3 %update_0.1.rest_0_ = f32[256,512,128]{2,1,0:T(8,128)} custom-call(f32[256,512,128]{2,1,0:T(8,128)} %z_ref.7, bf16[4,4,4,4,2,64,128]{6,5,4,3,2,1,0:T(8,128)(2,1)} %bitcast.64, f32[512,256]{1,0:T(8,128)} %fusion.29.inv_ref, f32[1,128]{1,0:T(1,128)} %bitcast_convert_fusion.1.b_ref), custom_call_target="tpu_custom_call" | custom-call | flops 30000001024 | bytes 40000000 | tf_op jit(solution)/shard_map/update_0/pallas_call | solution.py:59
  275.2 59.0 %all-gather.22.cloned.1.call-done = bf16[256,128,128]{2,1,0:T(8,128)(2,1)} async-done(((bf16[4,128,128]{2,1,0:T(8,128)(2,1)}), bf16[256,128,128]{2,1,0:T(8,128)(2,1)}) %all-gather.22.cloned.1.call-update) | async-done | bytes 8388624 | tf_op jit(solution)/shard_map/all_gather | solution.py:107
  334.3 21.3 %update_1.1.rest_0_ = f32[256,512,128]{2,1,0:T(8,128)} custom-call(f32[256,512,128]{2,1,0:T(8,128)} %z_ref.7, bf16[4,4,4,4,2,64,128]{6,5,4,3,2,1,0:T(8,128)(2,1)} %bitcast.65, f32[512,256]{1,0:T(8,128)} %fusion.29.inv_ref, f32[1,128]{1,0:T(1,128)} %bitcast_convert_fusion.1.b_ref, f32[256,512,128]{2,1,0:T(8,128)} %update_0.1.rest_0_), custom_call_target="tpu_custom_call", output_to_operand_aliasing={{}: (4, {})} | custom-call | flops 30000001024 | bytes 40000000 | tf_op jit(solution)/shard_map/update_1/pallas_call | solution.py:59
  355.6 59.1 %all-gather.20.cloned.1.call-done = bf16[256,128,128]{2,1,0:T(8,128)(2,1)} async-done(((bf16[4,128,128]{2,1,0:T(8,128)(2,1)}), bf16[256,128,128]{2,1,0:T(8,128)(2,1)}) %all-gather.20.cloned.1.call-update) | async-done | bytes 8388624 | tf_op jit(solution)/shard_map/all_gather | solution.py:107
  414.6 21.3 %update_2.1.rest_0_ = f32[256,512,128]{2,1,0:T(8,128)} custom-call(f32[256,512,128]{2,1,0:T(8,128)} %z_ref.7, bf16[4,4,4,4,2,64,128]{6,5,4,3,2,1,0:T(8,128)(2,1)} %bitcast.66, f32[512,256]{1,0:T(8,128)} %fusion.29.inv_ref, f32[1,128]{1,0:T(1,128)} %bitcast_convert_fusion.1.b_ref, f32[256,512,128]{2,1,0:T(8,128)} %update_1.1.rest_0_), custom_call_target="tpu_custom_call", output_to_operand_aliasing={{}: (4, {})} | custom-call | flops 30000001024 | bytes 40000000 | tf_op jit(solution)/shard_map/update_2/pallas_call | solution.py:59
  435.9 59.2 %all-gather.18.cloned.1.call-done = bf16[256,128,128]{2,1,0:T(8,128)(2,1)} async-done(((bf16[4,128,128]{2,1,0:T(8,128)(2,1)}), bf16[256,128,128]{2,1,0:T(8,128)(2,1)}) %all-gather.18.cloned.1.call-update) | async-done | bytes 8388624 | tf_op jit(solution)/shard_map/all_gather | solution.py:107
  495.1 21.3 %update_3.1 = f32[256,512,128]{2,1,0:T(8,128)} custom-call(f32[256,512,128]{2,1,0:T(8,128)} %z_ref.7, bf16[4,4,4,4,2,64,128]{6,5,4,3,2,1,0:T(8,128)(2,1)} %bitcast.67, f32[512,256]{1,0:T(8,128)} %fusion.29.inv_ref, f32[1,128]{1,0:T(1,128)} %bitcast_convert_fusion.1.b_ref, f32[256,512,128]{2,1,0:T(8,128)} %update_2.1.rest_0_), custom_call_target="tpu_custom_call", output_to_operand_aliasing={{}: (4, {})} | custom-call | flops 30000001024 | bytes 40000000 | tf_op jit(solution)/shard_map/update_3/pallas_call | solution.py:59
  (31 shorter events, 0.2 us)
Async XLA Ops:
  7.2 4.0 copy-start
  7.2 3.2 copy-start.4
  7.2 3.2 copy-start.5
  7.2 3.2 copy-start.6
  7.2 64.6 %all-gather.14.cloned.1.call-start = ((), (), s32[]{:S(2)}) async-start(), calls=%async_computation.5 | async-start | bytes 2621440 | tf_op jit(solution)/shard_map/all_gather | solution.py:91
  35.4 36.5 %copy-start.7 = (bf16[32]{0:T(256)(128)(2,1)S(1)}, bf16[32]{0:T(256)(128)(2,1)}, u32[]{:S(2)}) copy-start(bf16[32]{0:T(256)(128)(2,1)} %param.17) | copy-start | bytes 196
  35.4 36.5 %copy-start.3 = (bf16[64,32]{0,1:T(8,128)(2,1)S(1)}, bf16[64,32]{0,1:T(8,128)(2,1)}, u32[]{:S(2)}) copy-start(bf16[64,32]{0,1:T(8,128)(2,1)} %param.16) | copy-start | bytes 12292
  37.8 58.9 %all-gather.16.cloned.1.call-start = ((), (), s32[]{:S(2)}) async-start(), calls=%async_computation.6 | async-start | bytes 6291456 | tf_op jit(solution)/shard_map/all_gather | solution.py:92
  71.9 57.4 %all-gather.12.cloned.1.call-start = ((), (), s32[]{:S(2)}) async-start(), calls=%async_computation.4 | async-start | bytes 2621440 | tf_op jit(solution)/shard_map/all_gather | solution.py:89
  96.4 157.4 %all-gather.24.cloned.1.call-start = ((), (), s32[]{:S(2)}) async-start(), calls=%async_computation.10 | async-start | bytes 8519680 | tf_op jit(solution)/shard_map/all_gather | solution.py:107
  105.8 23.4 %copy-start.2 = (bf16[1024,128]{1,0:T(8,128)(2,1)S(1)}, bf16[1024,128]{1,0:T(8,128)(2,1)}, u32[]{:S(2)}) copy-start(bf16[1024,128]{1,0:T(8,128)(2,1)} %param.20) | copy-start | bytes 786436
  176.6 157.7 %all-gather.22.cloned.1.call-start = ((), (), s32[]{:S(2)}) async-start(), calls=%async_computation.9 | async-start | bytes 8519680 | tf_op jit(solution)/shard_map/all_gather | solution.py:107
  177.2 237.5 %all-gather.20.cloned.1.call-start = ((), (), s32[]{:S(2)}) async-start(), calls=%async_computation.8 | async-start | bytes 8519680 | tf_op jit(solution)/shard_map/all_gather | solution.py:107
  177.7 317.4 %all-gather.18.cloned.1.call-start = ((), (), s32[]{:S(2)}) async-start(), calls=%async_computation.7 | async-start | bytes 8519680 | tf_op jit(solution)/shard_map/all_gather | solution.py:107
  178.5 7.9 %all-to-all-start.3 = ((bf16[32,256,64]{1,2,0:T(8,128)(2,1)}), bf16[32,256,64]{1,2,0:T(8,128)(2,1)S(1)}, u32[]{:S(2)}, u32[]{:S(2)}) async-start(bf16[32,256,64]{1,2,0:T(8,128)(2,1)} %param.11), calls=%async_computation.3 | async-start | bytes 2097152 | tf_op jit(solution)/shard_map/all_to_all | solution.py:83
  186.4 2.6 copy-start.8
  495.1 21.3 %copy-start.1 = (bf16[64,32]{0,1:T(8,128)(2,1)S(1)}, bf16[64,32]{0,1:T(8,128)(2,1)}, u32[]{:S(2)}) copy-start(bf16[64,32]{0,1:T(8,128)(2,1)} %param.18) | copy-start | bytes 12292
Sparse Core Ops, SparseCore 0:
  37.9 33.8 all-gather.13
  73.5 17.4 all-gather.15
  96.6 32.5 all-gather.11
  176.7 77.1 all-gather.23
  256.6 77.6 all-gather.21
  337.0 77.6 all-gather.19
  417.5 77.6 all-gather.17

commit v2 on v1

--- a/solution.py
+++ b/solution.py
@@ -1,13 +1,9 @@
-import functools
-
 import jax
 import jax.numpy as jnp
 from jax import lax
 from jax.experimental import pallas as pl
 from jax.experimental.pallas import tpu as pltpu
 from jax.sharding import PartitionSpec as P
-
-CHUNKS = 4
 
 
 def layer_norm(value, ln_gamma, ln_beta):
@@ -25,47 +21,126 @@
     return (out_f32 * mask_f32[:, :, None]).astype(jnp.bfloat16)
 
 
-def update_kernel(rows, chunk, z_ref, g_ref, inv_ref, b_ref, *rest):
-    out_ref = rest[-1]
-    blk = pl.program_id(0) * 16 + pl.program_id(1) * 4 + chunk
-    shift = lax.rem(blk * rows, 128)
+AXES = ((2, 1, 0), (1, 0, 2), (0, 2, 1))
+SPLIT = (((0, 6), (6, 5)), ((11, 6), (17, 5)), ((22, 5), (27, 5)))
+
+
+def gather_kernel(t_ref, g_ref, send_sem, recv_sem, own_sem):
+    seq = lax.axis_index('seq')
+    me = (seq // 16, lax.rem(seq // 4, 4), lax.rem(seq, 4))
+    strides = (16, 4, 1)
+
+    def peer(axis, step):
+        pos = lax.rem(me[axis] + step + 4, 4)
+        return {'seq': seq + (pos - me[axis]) * strides[axis]}
+
+    barrier = pltpu.get_barrier_semaphore()
+    for axis in range(3):
+        for step in (1, -1):
+            pl.semaphore_signal(barrier, inc=1, device_id=peer(axis, step), device_id_type=pl.DeviceIdType.MESH)
+    pl.semaphore_wait(barrier, 6)
+
+    def block(part, phase, shift, u0, n):
+        idx = [pl.ds(me[a], 1) for a in range(3)]
+        for done in range(phase):
+            idx[AXES[part][done]] = pl.ds(0, 4)
+        axis = AXES[part][phase]
+        idx[axis] = pl.ds(lax.rem(me[axis] + shift + 4, 4), 1)
+        return g_ref.at[idx[0], idx[1], idx[2], pl.ds(u0, n)]
+
+    def message(c, part, phase, kind):
+        u0, n = SPLIT[part][c]
+        lo = (n + 1) // 2 if (part + c) % 2 == 0 else n // 2
+        if kind == 2:
+            n = lo
+        elif kind == 3:
+            u0, n = u0 + lo, n - lo
+        return u0, n
+
+    def copy(c, part, phase, kind, shift):
+        u0, n = message(c, part, phase, kind)
+        ref = block(part, phase, shift, u0, n)
+        src = ref
+        if phase == 0 and shift == 0:
+            src = t_ref.at[:, :, :, pl.ds(u0, n)]
+        return pltpu.make_async_remote_copy(
+            src_ref=src, dst_ref=ref, send_sem=send_sem.at[c, part, phase, kind],
+            recv_sem=recv_sem.at[c, part, phase, kind],
+            device_id=peer(AXES[part][phase], 1 if kind % 2 == 0 else -1),
+            device_id_type=pl.DeviceIdType.MESH)
+
+    sent_shift = (0, 0, -1, 1)
+    got_shift = (-1, 1, -2, 2)
+    own = pltpu.make_async_copy(t_ref, g_ref.at[pl.ds(me[0], 1), pl.ds(me[1], 1), pl.ds(me[2], 1)], own_sem)
+    order = [(c, p) for c in range(2) for p in range(3)]
+    for c, p in order:
+        copy(c, p, 0, 0, 0).start()
+        copy(c, p, 0, 1, 0).start()
+    own.start()
+    own.wait()
+    for phase in range(3):
+        for c, p in order:
+            for kind in (0, 1):
+                copy(c, p, phase, kind, got_shift[kind]).wait_recv()
+                copy(c, p, phase, kind + 2, sent_shift[kind + 2]).start()
+        for c, p in order:
+            for kind in (2, 3):
+                copy(c, p, phase, kind, got_shift[kind]).wait_recv()
+            if phase < 2:
+                copy(c, p, phase + 1, 0, 0).start()
+                copy(c, p, phase + 1, 1, 0).start()
+    for phase in range(3):
+        for c, p in order:
+            for kind in range(4):
+                copy(c, p, phase, kind, sent_shift[kind]).wait_send()
+
+
+def gather(tile):
+    return pl.pallas_call(
+        gather_kernel,
+        in_specs=[pl.BlockSpec(memory_space=pltpu.VMEM)],
+        out_specs=pl.BlockSpec(memory_space=pl.ANY),
+        out_shape=jax.ShapeDtypeStruct((4, 4, 4, 32, 64, 128), jnp.bfloat16),
+        scratch_shapes=[pltpu.SemaphoreType.DMA((2, 3, 3, 4)), pltpu.SemaphoreType.DMA((2, 3, 3, 4)), pltpu.SemaphoreType.DMA],
+        compiler_params=pltpu.CompilerParams(collective_id=1, has_side_effects=True),
+        name='gather_tiles',
+    )(tile.reshape(1, 1, 1, 32, 64, 128))
+
+
+ROWS = 8
+
+
+def update_kernel(z_ref, g_ref, inv_ref, b_ref, out_ref):
+    blk = (pl.program_id(0) * 4 + pl.program_id(1)) * (16 // ROWS) + pl.program_id(2)
+    shift = lax.rem(blk * ROWS, 128)
     inv = pltpu.roll(inv_ref[...], lax.rem(128 - shift, 128), 1)
     bias = b_ref[...]
-    for r in range(rows):
+    for r in range(ROWS):
         col = inv[:, r:r + 1]
         for h in range(2):
             for y in range(4):
                 j0 = h * 256 + y * 64
-                seg = g_ref[0, y, 0, r, h].astype(jnp.float32)
+                seg = g_ref[0, y, 0, 2 * r + h].astype(jnp.float32)
                 out_ref[r, j0:j0 + 64, :] = z_ref[r, j0:j0 + 64, :] + (seg + bias) * col[j0:j0 + 64]
 
 
-def update(chunk, n_chunks, pair_rows, gathered, inv_t, bias, prev):
-    rows = 16 // n_chunks
-    g = gathered.reshape(4, 4, 4, rows, 2, 64, 128)
-    row_map = lambda zi, xi: (zi * 16 + xi * 4 + chunk, 0, 0) if n_chunks == 4 else None
-    in_specs = [
-        pl.BlockSpec((rows, 512, 128), row_map),
-        pl.BlockSpec((1, 4, 1, rows, 2, 64, 128), lambda zi, xi: (zi, 0, xi, 0, 0, 0, 0)),
-        pl.BlockSpec((512, 128), lambda zi, xi: (0, (zi * 64 + xi * 16 + chunk * rows) // 128)),
-        pl.BlockSpec((1, 128), lambda zi, xi: (0, 0)),
-    ]
-    args = [pair_rows, g, inv_t, bias]
-    aliases = {}
-    if prev is not None:
-        in_specs.append(pl.BlockSpec(memory_space=pl.ANY))
-        args.append(prev)
-        aliases = {4: 0}
+def update(pair_rows, gathered, inv_t, bias):
+    nb = 16 // ROWS
+    row_map = lambda zi, xi, ri: ((zi * 4 + xi) * nb + ri, 0, 0)
     return pl.pallas_call(
-        functools.partial(update_kernel, rows, chunk),
-        grid=(4, 4),
-        in_specs=in_specs,
-        out_specs=pl.BlockSpec((rows, 512, 128), row_map),
+        update_kernel,
+        grid=(4, 4, nb),
+        in_specs=[
+            pl.BlockSpec((ROWS, 512, 128), row_map),
+            pl.BlockSpec((1, 4, 1, 2 * ROWS, 64, 128), lambda zi, xi, ri: (zi, 0, xi, ri, 0, 0)),
+            pl.BlockSpec((512, 128), lambda zi, xi, ri: (0, zi // 2)),
+            pl.BlockSpec((1, 128), lambda zi, xi, ri: (0, 0)),
+        ],
+        out_specs=pl.BlockSpec((ROWS, 512, 128), row_map),
         out_shape=jax.ShapeDtypeStruct(pair_rows.shape, jnp.float32),
-        input_output_aliases=aliases,
-        cost_estimate=pl.CostEstimate(flops=30_000_000_000, bytes_accessed=40_000_000, transcendentals=0),
-        name='update_%d' % chunk,
-    )(*args)
+        cost_estimate=pl.CostEstimate(flops=30_000_000_000, bytes_accessed=160_000_000, transcendentals=0),
+        name='update',
+    )(pair_rows, gathered, inv_t, bias)
 
 
 def solution(mesh):
@@ -103,11 +178,7 @@
         inv_t = 1.0 / (1e-3 + count_t)
         bias = b_out.astype(jnp.float32).reshape(1, 128)
 
-        rows = 16 // CHUNKS
-        gathered = [lax.all_gather(total[k * rows:(k + 1) * rows], 'seq', axis=0) for k in range(CHUNKS)]
-        out = None
-        for k in range(CHUNKS):
-            out = update(k, CHUNKS, pair_rows, gathered[k], inv_t, bias, out)
+        out = update(pair_rows, gather(total), inv_t, bias)
         return out, msa_out
 
     return jax.shard_map(local_fn, mesh=mesh, in_specs=in_specs, out_specs=out_specs, check_vma=False)

time: 526 us -> 380 us (0.72)
  waiting for transfers between devices: 292 us -> 60.8 us
  Pallas kernels: 85.3 us -> 196 us
  blocking collectives: 54.7 us -> 25.7 us
    all_gather x4 -> x0, waiting for transfers between devices: 238 us -> none  [local_fn(): lax.all_gather(total[k * rows:(k + 1) * rows], 'seq', axis=0)]
    pallas_call x4 -> x2, Pallas kernels: 85.3 us -> 196 us  [the longest x1 129 us: gather(): pl.pallas_call(gather_kernel, in_specs=[pl.BlockSpec(memory_space=pltpu.V...]
    all_to_all x1 -> x0, blocking collectives: 29 us -> none  [local_fn(): lax.all_to_all(partial.reshape(4, 16, 128, 128), 'seq', 0, 0, axis_index_...]
    all_to_all x0 -> x1, waiting for transfers between devices: none -> 12 us  [local_fn(): lax.all_to_all(partial.reshape(4, 16, 128, 128), 'seq', 0, 0, axis_index_...]
  transfers between devices with their start and end apart: 8 -> 5, of which waited for: 6 -> 3; matrix products, arithmetic and copies ran while one was open for 7% -> 14% of each run, Pallas kernels for 12% -> 0%
where the time goes in v2:
time: 380 us; the launch traced here: 379 us
  Pallas kernels  196 us (52%)
  waiting for transfers between devices  60.8 us (16%)
  local copies, waits for them, and re-layouts  40.5 us (11%)
  blocking collectives  25.7 us (7%)
  matrix products  24.3 us (6%)
  between operations  14 us (4%)
  other arithmetic  9.83 us (3%)
  starting transfers between devices  8.14 us (2%)
    pallas_call x1, Pallas kernels, gather(): pl.pallas_call(gather_kernel, in_specs=[pl.BlockSpec(memory_space=pltpu.V...  129 us
    pallas_call x1, Pallas kernels, update(): pl.pallas_call(update_kernel, grid=(4, 4, nb), in_specs=[pl.BlockSpec((RO...  66.8 us
    all_gather x1, waiting for transfers between devices, local_fn(): lax.all_gather(right, 'seq', axis=0, axis_index_groups=zgroups, tiled=True)  34 us
    dot_general x1, matrix products, local_fn(): jnp.einsum('icjd,cde->ije', outer, w3, preferred_element_type=jnp.float32)  17.1 us
    all_gather x1, waiting for transfers between devices, local_fn(): lax.all_gather(left, 'seq', axis=0, axis_index_groups=ygroups, tiled=True)  14.7 us
    all_to_all x1, blocking collectives, local_fn(): lax.all_to_all(right, 'seq', 1, 0, axis_index_groups=ygroups, tiled=True)  13.9 us
    all_to_all x1, waiting for transfers between devices, local_fn(): lax.all_to_all(partial.reshape(4, 16, 128, 128), 'seq', 0, 0, axis_index_...  12 us
    all_to_all x1, blocking collectives, local_fn(): lax.all_to_all(left, 'seq', 1, 0, axis_index_groups=zgroups, tiled=True)  11.8 us
  transfers between devices with their start and end apart: 5, of which 3 were waited for; matrix products, arithmetic and copies ran while one was open for 14% of the time, Pallas kernels for 0%

profile of v2, /device:TPU:0, one launch (start us, length us, event | category | flops | bytes accessed | tf_op | source)
XLA Modules:
  0.0 379.2 jit_solution(5189754103640832553)
XLA Ops:
  7.2 0.0 copy-start
  7.2 0.0 copy-start.4
  7.2 0.0 copy-start.5
  7.2 0.0 all-gather.6.cloned.1.call-start
  7.3 1.4 convert_reduce_fusion
  8.7 1.6 fusion.12
  10.4 0.0 copy-done.5
  10.4 0.8 dynamic-slice_convert_fusion
  11.2 1.8 fusion.27
  13.0 3.0 copy.33
  16.0 2.2 reshape.56
  18.2 13.9 %all_to_all.59 = bf16[4,2,32768]{2,1,0:T(2,128)(2,1)S(1)} all-to-all(bf16[4,2,32768]{2,1,0:T(2,128)(2,1)S(1)} %reshape.56), channel_id=1, replica_groups={{0,8,16,24},{2,10,18,26},{4,12,20,28},{6,14,22,30},{32,40,48,56},{34,42..., dimensions={0} | all-to-all | bytes 1048576 | tf_op jit(solution)/shard_map/all_to_all | solution.py:165
  32.1 1.1 reshape.57
  33.2 2.2 copy.34
  35.4 0.0 copy-start.7
  35.4 0.0 copy-start.3
  35.4 2.3 copy.35
  37.8 0.0 all-gather.6.cloned.1.call-update
  37.8 0.0 all-gather.8.cloned.1.call-start
  37.9 34.0 %all-gather.6.cloned.1.call-done = bf16[512,64,32]{0,2,1:T(8,128)(2,1)} async-done(((bf16[128,64,32]{0,2,1:T(8,128)(2,1)}), bf16[512,64,32]{0,2,1:T(8,128)(2,1)}) %all-gather.6.cloned.1.call-update) | async-done | bytes 2097168 | tf_op jit(solution)/shard_map/all_gather | solution.py:166
  71.8 0.0 all-gather.8.cloned.1.call-update
  71.9 0.0 all-gather.4.cloned.1.call-start
  71.9 1.8 fusion.26
  73.7 3.0 copy.30
  76.7 2.2 reshape.58
  79.0 11.8 %all_to_all.60 = bf16[4,2,32768]{2,1,0:T(2,128)(2,1)S(1)} all-to-all(bf16[4,2,32768]{2,1,0:T(2,128)(2,1)S(1)} %reshape.58), channel_id=1, replica_groups={{0,32,64,96},{2,34,66,98},{4,36,68,100},{6,38,70,102},{8,40,72,104},{10..., dimensions={0} | all-to-all | bytes 1048576 | tf_op jit(solution)/shard_map/all_to_all | solution.py:163
  90.8 1.1 reshape.59
  91.9 2.2 copy.31
  94.1 2.3 copy.32
  96.4 0.0 all-gather.4.cloned.1.call-update
  96.5 3.8 all-to-all-start.3
  100.2 0.0 all-gather.8.cloned.1.call-done
  100.3 9.1 %copy.36 = bf16[512,128,32]{1,2,0:T(8,128)(2,1)} copy(bf16[512,128,32]{0,2,1:T(8,128)(2,1)} %all-gather.8.cloned.1.call-done) | data formatting | bytes 8388608 | tf_op jit(solution)/shard_map/all_gather | solution.py:167
  109.4 5.1 %copy.37 = bf16[4,4,32,128,32]{3,4,2,1,0:T(8,128)(2,1)} copy(bf16[4,4,32,128,32]{3,4,2,0,1:T(8,128)(2,1)} %bitcast.60) | data formatting | bytes 8388608 | tf_op jit(solution)/shard_map/transpose | solution.py:168
  114.5 14.7 %all-gather.4.cloned.1.call-done = bf16[512,64,32]{0,2,1:T(8,128)(2,1)} async-done(((bf16[128,64,32]{0,2,1:T(8,128)(2,1)}), bf16[512,64,32]{0,2,1:T(8,128)(2,1)}) %all-gather.4.cloned.1.call-update) | async-done | bytes 2097168 | tf_op jit(solution)/shard_map/all_gather | solution.py:164
  129.2 17.1 %bitcast_convert_fusion = bf16[64,128,128]{2,1,0:T(8,128)(2,1)} fusion(bf16[512,128,32]{1,2,0:T(8,128)(2,1)} %bitcast.67, bf16[512,64,32]{0,2,1:T(8,128)(2,1)} %all-gather.4.cloned.1.call-done, bf16[32,32,128]{2,1,0:T(8,128)(2,1)S(1)} %bitcast.72), kind=kOutput, calls=%fused_computation.2 | convolution fusion | flops 10746855424 | bytes 8650752 | tf_op jit(solution)/shard_map/icjd,cde->ije/dot_general | solution.py:171
  146.3 0.0 all-to-all-done.3
  146.3 4.3 %all-to-all-start.2 = ((bf16[4,16,128,128]{3,2,1,0:T(8,128)(2,1)}), bf16[4,16,128,128]{3,2,1,0:T(8,128)(2,1)S(1)}, u32[]{:S(2)}, u32[]{:S(2)}) async-start(bf16[4,16,128,128]{3,2,1,0:T(8,128)(2,1)} %bitcast.71), calls=%async_computation.2 | async-start | bytes 4194304 | tf_op jit(solution)/shard_map/all_to_all | solution.py:172
  150.5 4.1 %convert_element_type.50 = bf16[2048,512]{1,0:T(8,128)(2,1)} convert(s32[2048,512]{1,0:T(8,128)} %param.12) | non-fusion elementwise | flops 1048576 | bytes 6291456 | tf_op jit(solution)/shard_map/convert_element_type | solution.py:175
  154.6 2.1 copy.57
  156.7 2.5 all_to_all.54
  159.2 0.6 bitcast_convert_fusion.1.b_ref
  159.8 3.7 fusion.29.inv_ref
  163.4 12.0 %all-to-all-done.2 = bf16[4,16,128,128]{3,2,1,0:T(8,128)(2,1)S(1)} async-done(((bf16[4,16,128,128]{3,2,1,0:T(8,128)(2,1)}), bf16[4,16,128,128]{3,2,1,0:T(8,128)(2,1)S(1)}, u32[]{:S(2)}, u32[]{:S(2)}) %all-to-all-start.2) | async-done | bytes 2097184 | tf_op jit(solution)/shard_map/all_to_all | solution.py:172
  175.5 1.3 reduce_sum.32
  176.8 129.1 %gather_tiles.1.g_ref = bf16[4,4,4,32,64,128]{5,4,3,2,1,0:T(8,128)(2,1)} custom-call(bf16[1,1,1,32,64,128]{5,4,3,2,1,0:T(8,128)(2,1)} %bitcast.70), custom_call_target="tpu_custom_call" | custom-call | tf_op jit(solution)/shard_map/gather_tiles/pallas_call | solution.py:99
  305.9 0.0 copy-start.1
  306.0 66.8 %update.1 = f32[256,512,128]{2,1,0:T(8,128)} custom-call(f32[256,512,128]{2,1,0:T(8,128)} %z_ref.1, bf16[4,4,4,32,64,128]{5,4,3,2,1,0:T(8,128)(2,1)} %gather_tiles.1.g_ref, f32[512,256]{1,0:T(8,128)} %fusion.29.inv_ref, f32[1,128]{1,0:T(1,128)} %bitcast_convert_fusion.1.b_ref), custom_call_target="tpu_custom_call" | custom-call | flops 30000001024 | bytes 160000000 | tf_op jit(solution)/shard_map/update/pallas_call | solution.py:130
  (17 shorter events, 0.1 us)
Async XLA Ops:
  7.2 4.0 %copy-start = (bf16[64,32]{0,1:T(8,128)(2,1)S(1)}, bf16[64,32]{0,1:T(8,128)(2,1)}, u32[]{:S(2)}) copy-start(bf16[64,32]{0,1:T(8,128)(2,1)} %param.18) | copy-start | bytes 12292
  7.2 3.2 copy-start.4
  7.2 3.2 copy-start.5
  7.2 3.2 copy-start.6
  7.2 64.6 %all-gather.6.cloned.1.call-start = ((), (), s32[]{:S(2)}) async-start(), calls=%async_computation.5 | async-start | bytes 2621440 | tf_op jit(solution)/shard_map/all_gather | solution.py:166
  35.4 36.5 %copy-start.7 = (bf16[32]{0:T(256)(128)(2,1)S(1)}, bf16[32]{0:T(256)(128)(2,1)}, u32[]{:S(2)}) copy-start(bf16[32]{0:T(256)(128)(2,1)} %param.17) | copy-start | bytes 196
  35.4 36.5 %copy-start.3 = (bf16[64,32]{0,1:T(8,128)(2,1)S(1)}, bf16[64,32]{0,1:T(8,128)(2,1)}, u32[]{:S(2)}) copy-start(bf16[64,32]{0,1:T(8,128)(2,1)} %param.16) | copy-start | bytes 12292
  37.8 62.5 %all-gather.8.cloned.1.call-start = ((), (), s32[]{:S(2)}) async-start(), calls=%async_computation.6 | async-start | bytes 6291456 | tf_op jit(solution)/shard_map/all_gather | solution.py:167
  71.9 57.4 %all-gather.4.cloned.1.call-start = ((), (), s32[]{:S(2)}) async-start(), calls=%async_computation.4 | async-start | bytes 2621440 | tf_op jit(solution)/shard_map/all_gather | solution.py:164
  96.5 49.8 %all-to-all-start.3 = ((bf16[32,256,64]{1,2,0:T(8,128)(2,1)}), bf16[32,256,64]{1,2,0:T(8,128)(2,1)S(1)}, u32[]{:S(2)}, u32[]{:S(2)}) async-start(bf16[32,256,64]{1,2,0:T(8,128)(2,1)} %param.11), calls=%async_computation.3 | async-start | bytes 2097152 | tf_op jit(solution)/shard_map/all_to_all | solution.py:158
  109.4 19.8 %copy-start.2 = (bf16[1024,128]{1,0:T(8,128)(2,1)S(1)}, bf16[1024,128]{1,0:T(8,128)(2,1)}, u32[]{:S(2)}) copy-start(bf16[1024,128]{1,0:T(8,128)(2,1)} %param.20) | copy-start | bytes 786436
  146.3 29.2 %all-to-all-start.2 = ((bf16[4,16,128,128]{3,2,1,0:T(8,128)(2,1)}), bf16[4,16,128,128]{3,2,1,0:T(8,128)(2,1)S(1)}, u32[]{:S(2)}, u32[]{:S(2)}) async-start(bf16[4,16,128,128]{3,2,1,0:T(8,128)(2,1)} %bitcast.71), calls=%async_computation.2 | async-start | bytes 4194304 | tf_op jit(solution)/shard_map/all_to_all | solution.py:172
  154.6 4.6 %copy-start.8 = (bf16[128]{0:T(256)(128)(2,1)S(1)}, bf16[128]{0:T(256)(128)(2,1)}, u32[]{:S(2)}) copy-start(bf16[128]{0:T(256)(128)(2,1)} %param.21) | copy-start | bytes 772
  305.9 66.8 %copy-start.1 = (bf16[64,32]{0,1:T(8,128)(2,1)S(1)}, bf16[64,32]{0,1:T(8,128)(2,1)}, u32[]{:S(2)}) copy-start(bf16[64,32]{0,1:T(8,128)(2,1)} %param.18) | copy-start | bytes 12292
Sparse Core Ops, SparseCore 0:
  37.9 33.8 all-gather.5
  73.5 17.4 all-gather.7
  96.6 32.5 all-gather.3

commit v3 on v2

--- a/solution.py
+++ b/solution.py
@@ -6,19 +6,215 @@
 from jax.sharding import PartitionSpec as P
 
 
-def layer_norm(value, ln_gamma, ln_beta):
-    act_f32 = value.astype(jnp.float32)
-    mean_val = jnp.mean(act_f32, axis=-1, keepdims=True)
-    centered = act_f32 - mean_val
-    var_val = jnp.mean(centered * centered, axis=-1, keepdims=True)
-    normed = centered * lax.rsqrt(var_val + 1e-5)
-    return (normed * ln_gamma.astype(jnp.float32) + ln_beta.astype(jnp.float32)).astype(jnp.bfloat16)
-
-
-def project(normed, weight, bias_vec, mask_f32):
-    out_f32 = jnp.einsum('sic,cd->sid', normed, weight, preferred_element_type=jnp.float32)
-    out_f32 = out_f32 + bias_vec.astype(jnp.float32)
-    return (out_f32 * mask_f32[:, :, None]).astype(jnp.bfloat16)
+STRIDE = 72
+
+
+def project_kernel(m_ref, mask_ref, gamma_ref, beta_ref, w_ref, bias_ref, a_ref, b_ref, scr):
+    gamma, beta, bias = gamma_ref[...], beta_ref[...], bias_ref[...]
+    w = w_ref[...]
+    for s in range(32):
+        x = m_ref[s].astype(jnp.float32)
+        cen = x - jnp.mean(x, axis=0, keepdims=True)
+        var = jnp.mean(cen * cen, axis=0, keepdims=True)
+        normed = (cen * lax.rsqrt(var + 1e-5) * gamma + beta).astype(jnp.bfloat16)
+        out = (jnp.dot(w, normed, preferred_element_type=jnp.float32) + bias) * mask_ref[s:s + 1, :]
+        for t in range(2):
+            scr[t, s * STRIDE:s * STRIDE + 64, :] = out[:, t * 128:t * 128 + 128]
+    low = lax.broadcasted_iota(jnp.int32, (32, 128), 1) < 64
+    for t in range(2):
+        for c in range(16):
+            lo = scr[t, pl.ds(c, 32, stride=STRIDE), :]
+            hi = scr[t, pl.ds(16 + c, 32, stride=STRIDE), :]
+            a_ref[2 * t, c] = jnp.where(low, lo, pltpu.roll(hi, 64, 1)).astype(jnp.bfloat16)
+            a_ref[2 * t + 1, c] = jnp.where(low, pltpu.roll(lo, 64, 1), hi).astype(jnp.bfloat16)
+        for d in range(32):
+            b_ref[d // 16, t, d % 16] = scr[t, pl.ds(32 + d, 32, stride=STRIDE), :].astype(jnp.bfloat16)
+
+
+def project(msa_t, mask_f32, gamma, beta, w_cat, bias_cat):
+    return pl.pallas_call(
+        project_kernel,
+        out_shape=(jax.ShapeDtypeStruct((4, 16, 32, 128), jnp.bfloat16), jax.ShapeDtypeStruct((2, 2, 16, 32, 128), jnp.bfloat16)),
+        scratch_shapes=[pltpu.VMEM((2, 32 * STRIDE, 128), jnp.float32)],
+        name='project',
+    )(msa_t, mask_f32, gamma, beta, w_cat, bias_cat)
+
+
+MESH = pl.DeviceIdType.MESH
+
+
+def exchange_kernel(a_in, b_in, a_out, b_out, b_mid, dap_sem, loc_sem, aa_send, aa_recv, bb_send, bb_recv, ag_send, ag_recv, bg_send, bg_recv, sib_send, sib_recv):
+    seq = lax.axis_index('seq')
+    core = lax.axis_index('dap')
+    z, y = seq // 16, lax.rem(seq // 4, 4)
+
+    def zpos(step):
+        return lax.rem(z + step + 4, 4)
+
+    def ypos(step):
+        return lax.rem(y + step + 4, 4)
+
+    def zpeer(step):
+        return {'seq': seq + (zpos(step) - z) * 16}
+
+    def ypeer(step):
+        return {'seq': seq + (ypos(step) - y) * 4}
+
+    sibling = {'dap': 1 - core}
+    barrier = pltpu.get_barrier_semaphore()
+    for peer in [zpeer(i) for i in (1, 2, 3)] + [ypeer(i) for i in (1, 2, 3)] + [sibling]:
+        pl.semaphore_signal(barrier, inc=1, device_id=peer, device_id_type=MESH)
+    pl.semaphore_wait(barrier, 7)
+
+    def remote(src, dst, ssem, rsem, peer):
+        return pltpu.make_async_remote_copy(src_ref=src, dst_ref=dst, send_sem=ssem, recv_sem=rsem, device_id=peer, device_id_type=MESH)
+
+    to_sib = remote(b_in.at[1 - core], b_mid.at[pl.ds(2 * core, 2)], dap_sem.at[0], dap_sem.at[1], sibling)
+    to_sib.start()
+    mine_b = pltpu.make_async_copy(b_in.at[core], b_mid.at[pl.ds(2 * core, 2)], loc_sem.at[0])
+    mine_b.start()
+    mine_a = pltpu.make_async_copy(a_in.at[z], a_out.at[:, y, z], loc_sem.at[1])
+    mine_a.start()
+
+    def a_scatter(shift):
+        return remote(a_in.at[zpos(shift)], a_out.at[:, y, z], aa_send.at[shift], aa_recv.at[shift], zpeer(shift))
+
+    def a_scattered(shift):
+        ref = a_out.at[:, y, zpos(-shift)]
+        return remote(ref, ref, aa_send.at[shift], aa_recv.at[shift], zpeer(shift))
+
+    def b_scatter(shift):
+        return remote(b_mid.at[ypos(shift)], b_out.at[core, :, y, z], bb_send.at[shift], bb_recv.at[shift], ypeer(shift))
+
+    def b_scattered(shift):
+        ref = b_out.at[core, :, ypos(-shift), z]
+        return remote(ref, ref, bb_send.at[shift], bb_recv.at[shift], ypeer(shift))
+
+    for shift in (1, 3, 2):
+        a_scatter(shift).start()
+    got = b_mid.at[pl.ds(2 * (1 - core), 2)]
+    remote(got, got, dap_sem.at[0], dap_sem.at[1], sibling).wait_recv()
+    mine_b.wait()
+    for shift in (1, 3, 2):
+        b_scatter(shift).start()
+    b_out[core, :, y, z] = b_mid[y]
+
+    half = ((0, 16), (0, 16), (0, 8), (8, 8))
+    shifts = (0, 0, -1, 1)
+    landed = (-1, 1, -2, 2)
+
+    def a_gather(kind, shift):
+        c0, n = half[kind]
+        ref = a_out.at[pl.ds(c0, n), ypos(shift)]
+        return remote(ref, ref, ag_send.at[kind], ag_recv.at[kind], ypeer(1 if kind % 2 == 0 else -1))
+
+    def b_gather(kind, shift):
+        c0, n = half[kind]
+        ref = b_out.at[core, pl.ds(c0, n), :, zpos(shift)]
+        return remote(ref, ref, bg_send.at[kind], bg_recv.at[kind], zpeer(1 if kind % 2 == 0 else -1))
+
+    def share(slot, which, shift, kind):
+        c0, n = half[kind]
+        ref = b_out.at[which, pl.ds(c0, n), :, zpos(shift)]
+        return remote(ref, ref, sib_send.at[slot], sib_recv.at[slot], sibling)
+
+    shared = ((0, 0), (-1, 0), (1, 0), (-2, 2), (2, 3))
+    for shift in (1, 3, 2):
+        a_scattered(shift).wait_recv()
+    mine_a.wait()
+    a_gather(0, 0).start()
+    a_gather(1, 0).start()
+    for shift in (1, 3, 2):
+        b_scattered(shift).wait_recv()
+    b_gather(0, 0).start()
+    b_gather(1, 0).start()
+    share(0, core, *shared[0]).start()
+    for kind in (0, 1):
+        a_gather(kind, landed[kind]).wait_recv()
+        a_gather(kind + 2, shifts[kind + 2]).start()
+        b_gather(kind, landed[kind]).wait_recv()
+        b_gather(kind + 2, shifts[kind + 2]).start()
+        share(kind + 1, core, *shared[kind + 1]).start()
+    for kind in (2, 3):
+        b_gather(kind, landed[kind]).wait_recv()
+        share(kind + 1, core, *shared[kind + 1]).start()
+    for kind in (2, 3):
+        a_gather(kind, landed[kind]).wait_recv()
+    for slot in range(5):
+        share(slot, 1 - core, *shared[slot]).wait_recv()
+    to_sib.wait_send()
+    for shift in (1, 3, 2):
+        a_scatter(shift).wait_send()
+        b_scatter(shift).wait_send()
+    for kind in range(4):
+        a_gather(kind, shifts[kind]).wait_send()
+        b_gather(kind, shifts[kind]).wait_send()
+    for slot in range(5):
+        share(slot, core, *shared[slot]).wait_send()
+
+
+def exchange(a_loc, b_loc):
+    dma = pltpu.SemaphoreType.DMA
+    return pl.pallas_call(
+        exchange_kernel,
+        in_specs=[pl.BlockSpec(memory_space=pl.ANY)] * 2,
+        out_specs=(pl.BlockSpec(memory_space=pltpu.VMEM),) * 2,
+        out_shape=(jax.ShapeDtypeStruct((16, 4, 4, 32, 128), jnp.bfloat16), jax.ShapeDtypeStruct((2, 16, 4, 4, 32, 128), jnp.bfloat16)),
+        scratch_shapes=[pltpu.VMEM((4, 16, 32, 128), jnp.bfloat16), dma((2,)), dma((2,))] + [dma((4,))] * 8 + [dma((5,))] * 2,
+        compiler_params=pltpu.CompilerParams(collective_id=2, has_side_effects=True),
+        name='exchange',
+    )(a_loc, b_loc)
+
+
+def pair_kernel(a_ref, b_ref, w_ref, out_ref, at_f32, at, outer):
+    def transpose_a(c, _):
+        for sb in range(4):
+            blk = a_ref[c, sb * 128:sb * 128 + 128, :].astype(jnp.float32).T
+            at_f32[sb, pl.ds(pl.multiple_of(c * STRIDE, 8), 64), :] = blk[:64]
+            at_f32[sb, pl.ds(pl.multiple_of((c + 16) * STRIDE, 8), 64), :] = blk[64:]
+        return 0
+
+    lax.fori_loop(0, 16, transpose_a, 0)
+
+    def regroup(i, _):
+        for sb in range(4):
+            rows = at_f32[sb, pl.ds(i, 32, stride=STRIDE), :]
+            at[pl.ds(pl.multiple_of(i * 32, 32), 32), sb * 128:sb * 128 + 128] = rows.astype(jnp.bfloat16)
+        return 0
+
+    lax.fori_loop(0, 64, regroup, 0, unroll=2)
+
+    def products(dp, _):
+        rhs = jnp.concatenate([b_ref[2 * dp], b_ref[2 * dp + 1]], axis=1)
+        for mc in range(4):
+            prod = jnp.dot(at[mc * 512:mc * 512 + 512, :], rhs, preferred_element_type=jnp.float32).astype(jnp.bfloat16)
+            for i in range(16):
+                for dd in range(2):
+                    row = pl.multiple_of((2 * dp + dd) * 32, 32)
+                    lane = (i % 2) * 128
+                    outer[mc * 8 + i // 2, pl.ds(row, 32), lane:lane + 128] = prod[i * 32:i * 32 + 32, dd * 128:dd * 128 + 128]
+        return 0
+
+    lax.fori_loop(0, 16, products, 0)
+    w = w_ref[...]
+
+    def combine(ip, _):
+        res = jnp.dot(w, outer[ip], preferred_element_type=jnp.float32)
+        out_ref[2 * ip] = res[:, :128].T.astype(jnp.bfloat16)
+        out_ref[2 * ip + 1] = res[:, 128:].T.astype(jnp.bfloat16)
+        return 0
+
+    lax.fori_loop(0, 32, combine, 0, unroll=2)
+
+
+def pair_partial(a_full, b_full, w2):
+    return pl.pallas_call(
+        pair_kernel,
+        out_shape=jax.ShapeDtypeStruct((64, 128, 128), jnp.bfloat16),
+        scratch_shapes=[pltpu.VMEM((4, 32 * STRIDE, 128), jnp.float32), pltpu.VMEM((2048, 512), jnp.bfloat16), pltpu.VMEM((32, 1024, 256), jnp.bfloat16)],
+        cost_estimate=pl.CostEstimate(flops=12_000_000_000, bytes_accessed=8_000_000, transcendentals=0),
+        name='pair_partial',
+    )(a_full.reshape(16, 512, 128), b_full.reshape(32, 512, 128), w2)
 
 
 AXES = ((2, 1, 0), (1, 0, 2), (0, 2, 1))
@@ -119,7 +315,7 @@
         col = inv[:, r:r + 1]
         for h in range(2):
             for y in range(4):
-                j0 = h * 256 + y * 64
+                j0 = y * 128 + h * 64
                 seg = g_ref[0, y, 0, 2 * r + h].astype(jnp.float32)
                 out_ref[r, j0:j0 + 64, :] = z_ref[r, j0:j0 + 64, :] + (seg + bias) * col[j0:j0 + 64]
 
@@ -148,8 +344,6 @@
     in_specs = (P(('data', 'seq'), 'dap', None), P('data', None), P(('data', 'dap'), None, None)) + (rep,) * 8
     out_specs = (P(('data', 'dap'), None, None), P(('data', 'seq', 'dap'), None, None))
     rng = range(4)
-    zgroups = [[z * 16 + y * 4 + x for z in rng] for y in rng for x in rng]
-    ygroups = [[z * 16 + y * 4 + x for y in rng] for z in rng for x in rng]
     xgroups = [[z * 16 + y * 4 + x for x in rng] for z in rng for y in rng]
 
     def local_fn(msa, mask, pair_rows, ln_gamma, ln_beta, w_left, b_left, w_right, b_right, w_out, b_out):
@@ -157,18 +351,13 @@
         dap_idx = lax.axis_index('dap')
         msa_out = lax.all_to_all(msa, 'dap', 0, 1, tiled=True)
         mask_seq = lax.dynamic_slice(mask, (seq_idx * 32, dap_idx * 256), (32, 256)).astype(jnp.float32)
-        normed = layer_norm(msa, ln_gamma, ln_beta)
-        left = project(normed, w_left, b_left, mask_seq)
-        right = project(normed, w_right, b_right, mask_seq)
-        left = lax.all_to_all(left, 'seq', 1, 0, axis_index_groups=zgroups, tiled=True)
-        left = lax.all_gather(left, 'seq', axis=0, axis_index_groups=ygroups, tiled=True)
-        right = lax.all_to_all(right, 'seq', 1, 0, axis_index_groups=ygroups, tiled=True)
-        right = lax.all_gather(right, 'seq', axis=0, axis_index_groups=zgroups, tiled=True)
-        right = lax.all_gather(right, 'dap', axis=1, tiled=True)
-        right = right.reshape(4, 4, 32, 128, 32).transpose(1, 0, 2, 3, 4).reshape(512, 128, 32)
-        w3 = w_out.reshape(32, 32, 128)
-        outer = jnp.einsum('sic,sjd->icjd', left, right, preferred_element_type=jnp.float32).astype(jnp.bfloat16)
-        partial = jnp.einsum('icjd,cde->ije', outer, w3, preferred_element_type=jnp.float32).astype(jnp.bfloat16)
+        col = lambda v: v.astype(jnp.float32).reshape(-1, 1)
+        w_cat = jnp.concatenate([w_left, w_right], axis=1).T
+        bias_cat = jnp.concatenate([col(b_left), col(b_right)], axis=0)
+        a_loc, b_loc = project(jnp.swapaxes(msa, 1, 2), mask_seq, col(ln_gamma), col(ln_beta), w_cat, bias_cat)
+        a_full, b_full = exchange(a_loc, b_loc)
+        w2 = w_out.reshape(32, 32, 128).transpose(2, 1, 0).reshape(128, 1024)
+        partial = pair_partial(a_full, b_full, w2)
         parts = lax.all_to_all(partial.reshape(4, 16, 128, 128), 'seq', 0, 0, axis_index_groups=xgroups, tiled=True)
         total = jnp.sum(parts.astype(jnp.float32), axis=0).astype(jnp.bfloat16)
 

time: 380 us -> 308 us (0.81)
  Pallas kernels: 196 us -> 266 us
  waiting for transfers between devices: 60.8 us -> 14 us
  local copies, waits for them, and re-layouts: 40.5 us -> 7.66 us
  blocking collectives: 25.7 us -> 0 us
  matrix products: 24.3 us -> 3.67 us
  between operations: 14 us -> 0.75 us
    pallas_call x0 -> x3, Pallas kernels: none -> 68.1 us  [the longest x1 39.2 us: exchange(): pl.pallas_call(exchange_kernel, in_specs=[pl.BlockSpec(memory_space=pl.AN...]
    all_gather x3 -> x0, waiting for transfers between devices: 48.7 us -> none  [the longest x1 34 us: local_fn(): lax.all_gather(right, 'seq', axis=0, axis_index_groups=zgroups, tiled=True)]
    all_to_all x2 -> x0, blocking collectives: 25.7 us -> none  [the longest x1 13.9 us: local_fn(): lax.all_to_all(right, 'seq', 1, 0, axis_index_groups=ygroups, tiled=True)]
    dot_general x3 -> x0, matrix products: 20.6 us -> none  [the longest x1 17.1 us: local_fn(): jnp.einsum('icjd,cde->ije', outer, w3, preferred_element_type=jnp.float32)]
    all_gather x1 -> x0, local copies, waits for them, and re-layouts: 9.13 us -> none  [local_fn(): right = lax.all_gather(right, 'dap', axis=1, tiled=True)]
    all_to_all x4 -> x0, local copies, waits for them, and re-layouts: 9.06 us -> none  [the longest x2 4.53 us: local_fn(): lax.all_to_all(left, 'seq', 1, 0, axis_index_groups=zgroups, tiled=True)]
    unnamed x22 -> x16, local copies, waits for them, and re-layouts: 6.65 us -> 0.03 us
    convert_element_type x2 -> x0, local copies, waits for them, and re-layouts: 6.01 us -> none  [project(): return (out_f32 * mask_f32[:, :, None]).astype(jnp.bfloat16)]
  transfers between devices with their start and end apart: 5 -> 2, of which waited for: 3 -> 1; matrix products, arithmetic and copies ran while one was open for 14% -> 5% of each run, Pallas kernels for 0% -> 22%
where the time goes in v3:
time: 308 us
  Pallas kernels  266 us (86%)
  waiting for transfers between devices  14 us (5%)
  starting transfers between devices  8.03 us (3%)
  other arithmetic  7.96 us (3%)
  local copies, waits for them, and re-layouts  7.66 us (2%)
  matrix products  3.67 us (1%)
    pallas_call x1, Pallas kernels, gather(): pl.pallas_call(gather_kernel, in_specs=[pl.BlockSpec(memory_space=pltpu.V...  131 us
    pallas_call x1, Pallas kernels, update(): pl.pallas_call(update_kernel, grid=(4, 4, nb), in_specs=[pl.BlockSpec((RO...  67.1 us
    pallas_call x1, Pallas kernels, exchange(): pl.pallas_call(exchange_kernel, in_specs=[pl.BlockSpec(memory_space=pl.AN...  39.2 us
    pallas_call x1, Pallas kernels, pair_partial(): pl.pallas_call(pair_kernel, out_shape=jax.ShapeDtypeStruct((64, 128, 128)...  25.3 us
    all_to_all x1, waiting for transfers between devices, local_fn(): lax.all_to_all(partial.reshape(4, 16, 128, 128), 'seq', 0, 0, axis_index_...  14 us
  transfers between devices with their start and end apart: 2, of which 1 were waited for; matrix products, arithmetic and copies ran while one was open for 5% of the time, Pallas kernels for 22%

profile of v3, /device:TPU:0, one launch (start us, length us, event | category | flops | bytes accessed | tf_op | source)
XLA Modules:
  0.0 307.8 jit_solution(5097536784152997562)
XLA Ops:
  0.6 0.0 copy-start.3
  0.6 0.0 copy-start.4
  0.7 0.0 copy-start.6
  0.7 0.0 copy-start.5
  0.7 0.0 copy-start
  0.7 0.0 copy-start.2
  0.7 0.0 copy-start.1
  0.7 3.7 %all-to-all-start.1 = ((bf16[32,256,64]{1,2,0:T(8,128)(2,1)}), bf16[32,256,64]{1,2,0:T(8,128)(2,1)S(1)}, u32[]{:S(2)}, u32[]{:S(2)}) async-start(bf16[32,256,64]{1,2,0:T(8,128)(2,1)} %param.11), calls=%async_computation.1 | async-start | bytes 2097152 | tf_op jit(solution)/shard_map/all_to_all | solution.py:352
  4.4 0.0 copy-done.3
  4.5 0.7 copy.42.gamma_ref
  5.2 0.0 copy-done.4
  5.2 0.7 copy.43.beta_ref
  5.9 0.0 copy-done.6
  5.9 0.0 copy-done.5
  5.9 0.1 maximum_convert_fusion
  5.9 0.7 copy.44.bias_ref
  6.6 0.0 copy-done
  6.6 0.1 copy.45
  6.8 0.8 copy.46.w_ref
  7.6 0.0 copy-done.2
  7.6 0.0 copy-done.1
  7.6 0.6 maximum_bitcast_fusion.w_ref
  8.2 1.4 dynamic-slice_convert_fusion.mask_ref
  9.6 3.7 %project.1 = (bf16[4,16,32,128]{3,2,1,0:T(8,128)(2,1)}, bf16[2,2,16,32,128]{4,3,2,1,0:T(8,128)(2,1)}) custom-call(bf16[32,64,256]{2,1,0:T(8,128)(2,1)} %bitcast.31, f32[32,256]{1,0:T(8,128)} %dynamic-slice_convert_fusion.mask_ref, f32[64,1]{1,0:T(8,128)} %copy.42.gamma_ref, f32[64,1]{1,0:T(8,128)} %copy.43.beta_ref, ...), custom_call_target="tpu_custom_call" | custom-call | tf_op jit(solution)/shard_map/project/pallas_call | solution.py:35
  13.2 39.2 %exchange.1 = (bf16[16,4,4,32,128]{4,3,2,1,0:T(8,128)(2,1)}, bf16[2,16,4,4,32,128]{5,4,3,2,1,0:T(8,128)(2,1)}) custom-call(bf16[4,16,32,128]{3,2,1,0:T(8,128)(2,1)} %get-tuple-element.6.a_in, bf16[2,2,16,32,128]{4,3,2,1,0:T(8,128)(2,1)} %get-tuple-element.7.b_in), custom_call_target="tpu_custom_call" | custom-call | tf_op jit(solution)/shard_map/exchange/pallas_call | solution.py:158
  52.4 25.3 %pair_partial.1 = bf16[64,128,128]{2,1,0:T(8,128)(2,1)} custom-call(bf16[16,512,128]{2,1,0:T(8,128)(2,1)} %bitcast.39, bf16[32,512,128]{2,1,0:T(8,128)(2,1)} %bitcast.38, bf16[128,1024]{1,0:T(8,128)(2,1)} %copy.46.w_ref), custom_call_target="tpu_custom_call" | custom-call | flops 12000000000 | bytes 8000000 | tf_op jit(solution)/shard_map/pair_partial/pallas_call | solution.py:211
  77.7 0.0 all-to-all-done.1
  77.7 4.3 %all-to-all-start = ((bf16[4,16,128,128]{3,2,1,0:T(8,128)(2,1)}), bf16[4,16,128,128]{3,2,1,0:T(8,128)(2,1)S(1)}, u32[]{:S(2)}, u32[]{:S(2)}) async-start(bf16[4,16,128,128]{3,2,1,0:T(8,128)(2,1)} %bitcast.35), calls=%async_computation | async-start | bytes 4194304 | tf_op jit(solution)/shard_map/all_to_all | solution.py:361
  82.0 4.1 %convert_element_type.5 = bf16[2048,512]{1,0:T(8,128)(2,1)} convert(s32[2048,512]{1,0:T(8,128)} %param.12) | non-fusion elementwise | flops 1048576 | bytes 6291456 | tf_op jit(solution)/shard_map/convert_element_type | solution.py:364
  86.1 0.0 copy-start.7
  86.1 2.1 copy.51
  88.2 2.5 all_to_all.20
  90.7 0.0 copy-done.7
  90.7 0.5 bitcast_convert_fusion.b_ref
  91.2 3.7 %fusion.1.inv_ref = f32[512,256]{1,0:T(8,128)} fusion(bf16[2048,512]{1,0:T(8,128)(2,1)} %convert_element_type.5, s32[]{:T(128)S(6)} %select_n.8), kind=kOutput, calls=%fused_computation.2 | convolution fusion | flops 537133056 | bytes 3670020 | tf_op jit(solution)/shard_map/sj,si->ji/dot_general | solution.py:366
  94.9 14.0 %all-to-all-done = bf16[4,16,128,128]{3,2,1,0:T(8,128)(2,1)S(1)} async-done(((bf16[4,16,128,128]{3,2,1,0:T(8,128)(2,1)}), bf16[4,16,128,128]{3,2,1,0:T(8,128)(2,1)S(1)}, u32[]{:S(2)}, u32[]{:S(2)}) %all-to-all-start) | async-done | bytes 2097184 | tf_op jit(solution)/shard_map/all_to_all | solution.py:361
  108.9 1.3 reduce_sum.12
  110.2 130.6 %gather_tiles.1.g_ref = bf16[4,4,4,32,64,128]{5,4,3,2,1,0:T(8,128)(2,1)} custom-call(bf16[1,1,1,32,64,128]{5,4,3,2,1,0:T(8,128)(2,1)} %bitcast.34), custom_call_target="tpu_custom_call" | custom-call | tf_op jit(solution)/shard_map/gather_tiles/pallas_call | solution.py:295
  240.8 67.1 %update.1 = f32[256,512,128]{2,1,0:T(8,128)} custom-call(f32[256,512,128]{2,1,0:T(8,128)} %z_ref.1, bf16[4,4,4,32,64,128]{5,4,3,2,1,0:T(8,128)(2,1)} %gather_tiles.1.g_ref, f32[512,256]{1,0:T(8,128)} %fusion.1.inv_ref, f32[1,128]{1,0:T(1,128)} %bitcast_convert_fusion.b_ref), custom_call_target="tpu_custom_call" | custom-call | flops 30000001024 | bytes 160000000 | tf_op jit(solution)/shard_map/update/pallas_call | solution.py:326
  (2 shorter events, 0.0 us)
Async XLA Ops:
  0.6 3.8 %copy-start.3 = (bf16[64]{0:T(256)(128)(2,1)S(1)}, bf16[64]{0:T(256)(128)(2,1)}, u32[]{:S(2)}) copy-start(bf16[64]{0:T(256)(128)(2,1)} %param.14) | copy-start | bytes 388
  0.6 4.5 %copy-start.4 = (bf16[64]{0:T(256)(128)(2,1)S(1)}, bf16[64]{0:T(256)(128)(2,1)}, u32[]{:S(2)}) copy-start(bf16[64]{0:T(256)(128)(2,1)} %param.15) | copy-start | bytes 388
  0.7 5.2 %copy-start.6 = (bf16[32]{0:T(256)(128)(2,1)S(1)}, bf16[32]{0:T(256)(128)(2,1)}, u32[]{:S(2)}) copy-start(bf16[32]{0:T(256)(128)(2,1)} %param.17) | copy-start | bytes 196
  0.7 5.2 %copy-start.5 = (bf16[32]{0:T(256)(128)(2,1)S(1)}, bf16[32]{0:T(256)(128)(2,1)}, u32[]{:S(2)}) copy-start(bf16[32]{0:T(256)(128)(2,1)} %param.19) | copy-start | bytes 196
  0.7 6.0 %copy-start = (bf16[1024,128]{1,0:T(8,128)(2,1)S(1)}, bf16[1024,128]{1,0:T(8,128)(2,1)}, u32[]{:S(2)}) copy-start(bf16[1024,128]{1,0:T(8,128)(2,1)} %param.20) | copy-start | bytes 786436
  0.7 6.9 %copy-start.2 = (bf16[64,32]{0,1:T(8,128)(2,1)S(1)}, bf16[64,32]{0,1:T(8,128)(2,1)}, u32[]{:S(2)}) copy-start(bf16[64,32]{0,1:T(8,128)(2,1)} %param.16) | copy-start | bytes 12292
  0.7 6.9 %copy-start.1 = (bf16[64,32]{0,1:T(8,128)(2,1)S(1)}, bf16[64,32]{0,1:T(8,128)(2,1)}, u32[]{:S(2)}) copy-start(bf16[64,32]{0,1:T(8,128)(2,1)} %param.18) | copy-start | bytes 12292
  0.7 77.0 %all-to-all-start.1 = ((bf16[32,256,64]{1,2,0:T(8,128)(2,1)}), bf16[32,256,64]{1,2,0:T(8,128)(2,1)S(1)}, u32[]{:S(2)}, u32[]{:S(2)}) async-start(bf16[32,256,64]{1,2,0:T(8,128)(2,1)} %param.11), calls=%async_computation.1 | async-start | bytes 2097152 | tf_op jit(solution)/shard_map/all_to_all | solution.py:352
  77.7 31.2 %all-to-all-start = ((bf16[4,16,128,128]{3,2,1,0:T(8,128)(2,1)}), bf16[4,16,128,128]{3,2,1,0:T(8,128)(2,1)S(1)}, u32[]{:S(2)}, u32[]{:S(2)}) async-start(bf16[4,16,128,128]{3,2,1,0:T(8,128)(2,1)} %bitcast.35), calls=%async_computation | async-start | bytes 4194304 | tf_op jit(solution)/shard_map/all_to_all | solution.py:361
  86.1 4.6 %copy-start.7 = (bf16[128]{0:T(256)(128)(2,1)S(1)}, bf16[128]{0:T(256)(128)(2,1)}, u32[]{:S(2)}) copy-start(bf16[128]{0:T(256)(128)(2,1)} %param.21) | copy-start | bytes 772
